TPU v7x, 32 devices: a whole 2x2x4 slice. The times are simulated.
32 devices in a mesh: grid: 8 (over y, x, core), sub: 4 (over z).
Axes of the slice: x: 2, y: 2, z: 4, core: 2. Of those that a mesh axis runs over, the one named last changes fastest.
Arguments:
- grid_x: bfloat16 [65536, 512], P(('grid', 'sub')), may hold values from -6 to 6
- mesh_h: bfloat16 [2048, 512], P(('grid', 'sub')), may hold values from -6 to 6
- gain_grid: float32 [512], replicated, may hold values from 0.1 to 1.9
- gain_mesh: float32 [512], replicated, may hold values from 0.1 to 1.9
- w_query: bfloat16 [512, 512], replicated, may hold values from -0.25 to 0.25
- w_key: bfloat16 [512, 512], replicated, may hold values from -0.25 to 0.25
- w_value: bfloat16 [512, 512], replicated, may hold values from -0.25 to 0.25
- w_out: bfloat16 [512, 512], replicated, may hold values from -0.25 to 0.25
- edge_bias: float32 [2048, 384], P(('grid', 'sub')), may hold values from -9 to 300
- neighbours: int32 [2048, 96], P(('grid', 'sub')), may hold values from 0 to 767, as said below
- valid: int32 [2048, 96], P(('grid', 'sub')), may hold values from 0 to 1, as said below
- send_rows: int32 [32, 3, 4, 64], P(('grid', 'sub')), may hold values from 0 to 2047, as said below
- out_grad: bfloat16 [2048, 512], P(('grid', 'sub')), may hold values from -24 to 24
Outputs:
- mesh_out: bfloat16 [2048, 512], P(('grid', 'sub'))
- mesh_grad: bfloat16 [2048, 512], P(('grid', 'sub'))
- grid_grad: bfloat16 [65536, 512], P(('grid', 'sub'))
- weight_grads: float32 [4, 512, 512], replicated
Inputs may be any that keep to these rules, and one draw needn't show every extreme that they name: `send_rows`: for each source device, slab offset and destination sub index the 64 local rows are distinct; rows sent to the slab below (o = 0) lie in the lower half of the device's 2048 rows, rows sent to the slab above (o = 2) in the upper half. `neighbours`: a slot (o * 4 + s) * 64 + t names row t of what device s of slab g - o + 1 sends to the node's device; slots of slabs outside the grid are never named; the 96 entries of a node are distinct; some slots are named by no node. The first two edges of every node are valid.
All inputs are finite; a program needn't handle non-finite values.
Results may differ from a plain program's by a relative error of at most 0.009.
Values may be sent and summed in bfloat16 or wider, within the bound.
A program may use at most 128 MiB of HBM per device.

v0:
```python
import functools

import jax
import jax.numpy as jnp
from jax import lax
from jax.experimental import pallas as pl
from jax.sharding import PartitionSpec as P

EPSILON = 1e-06
NEG_FILL = -1e30


def from_behind(block, axis, distance):
    devices = range(lax.axis_size(axis))
    route = [(i - distance, i) for i in devices if i - distance in devices]
    return lax.ppermute(block, axis, route)


def normalize(values_in, gain_row):
    widened = values_in.astype(jnp.float32)
    factor = lax.rsqrt(jnp.mean(widened * widened, axis=-1, keepdims=True) + EPSILON)
    return (widened, factor, (widened * factor * gain_row).astype(jnp.bfloat16))


def normalize_back(widened, factor, gain_row, upstream):
    scaled = gain_row * upstream
    inner_mean = jnp.mean(widened * scaled, axis=-1, keepdims=True)
    return factor * scaled - widened * factor**3 * inner_mean


def spread_edges(nbr_ref, rows_ref, out_ref):
    slots = out_ref.shape[2]
    fanout = nbr_ref.shape[1]
    slot_ids = lax.broadcasted_iota(jnp.int32, (slots, fanout), 0)
    for node in range(nbr_ref.shape[0]):
        names = slot_ids == nbr_ref[pl.ds(node, 1), :]
        onehot = jnp.where(names, 1.0, 0.0).astype(jnp.bfloat16)
        spread = lax.dot_general(
            rows_ref[node], onehot, (((1,), (1,)), ((), ())), preferred_element_type=jnp.float32
        )
        out_ref[node] = (spread[16:24] + spread[8:16]) + spread[:8]


def attend(scale, q_ref, k_ref, v_ref, ag_ref, bias_ref, live_ref, att_ref, qg_ref, back_ref):
    queries, keys, values, att_grad = q_ref[...], k_ref[...], v_ref[...], ag_ref[...]
    nt = (((1,), (1,)), ((), ()))
    tn = (((0,), (0,)), ((), ()))

    def dot(a, b, dims):
        return lax.dot_general(a, b, dims, preferred_element_type=jnp.float32)

    live = live_ref[0] > 0.5
    scores = dot(queries, keys, nt) + bias_ref[0]
    peak = jnp.max(jnp.where(live, scores, NEG_FILL), axis=1, keepdims=True)
    terms = jnp.exp(jnp.where(live, scores - peak, NEG_FILL))
    probs = terms / jnp.sum(terms, axis=1, keepdims=True)
    probs_b = probs.astype(jnp.bfloat16)
    nn = (((1,), (0,)), ((), ()))
    att_ref[...] = dot(probs_b, values, nn).astype(jnp.bfloat16)
    prob_grads = dot(att_grad, values, nt)
    score_grads = (
        probs * (prob_grads - jnp.sum(probs * prob_grads, axis=1, keepdims=True))
    ).astype(jnp.bfloat16)
    qg_ref[...] = (dot(score_grads, keys, nn) * scale).astype(jnp.bfloat16)
    back_ref[0] = dot(score_grads, queries, tn).astype(jnp.bfloat16)
    back_ref[1] = dot(probs_b, att_grad, tn).astype(jnp.bfloat16)


def reduce_weights(local_grads):
    return lax.psum(local_grads, ("grid", "sub"))


def shards(
    grid_x,
    mesh_h,
    gain_grid,
    gain_mesh,
    w_query,
    w_key,
    w_value,
    w_out,
    edge_bias,
    neighbours,
    valid,
    send_rows,
    out_grad,
):
    point_count, model_width = grid_x.shape
    node_count = mesh_h.shape[0]
    sub_count = send_rows.shape[2]
    slots_per = send_rows.shape[3]
    block = sub_count * slots_per
    slot_count = 3 * block
    fanout = neighbours.shape[1]
    head_count = edge_bias.shape[1] // fanout
    head_width = model_width // head_count
    logit_scale = head_width ** (-0.5)
    w_pair = jnp.concatenate([w_key, w_value], axis=1)
    grid_wide, grid_factor, grid_normed = normalize(grid_x, gain_grid)
    flat_rows = send_rows[0].reshape(slot_count)
    send_match = flat_rows[:, None] == jnp.arange(point_count, dtype=jnp.int32)[None, :]
    send_onehot = send_match.astype(jnp.bfloat16)
    sent_normed = jnp.dot(send_onehot, grid_normed, preferred_element_type=jnp.float32).astype(
        jnp.bfloat16
    )
    packet = sent_normed.reshape(3, sub_count, slots_per, model_width)
    packet_width = packet.shape[3]
    mixed = lax.all_to_all(packet, "sub", split_axis=1, concat_axis=1, tiled=True).reshape(
        3, block, packet_width
    )
    pieces = []
    for offset in (0, 1, 2):
        piece = mixed[offset]
        if offset != 1:
            piece = from_behind(piece, "grid", offset - 1)
        pieces.append(piece)
    arrived = jnp.concatenate(pieces, axis=0)
    recv_pair = jnp.dot(arrived, w_pair, preferred_element_type=jnp.float32).astype(jnp.bfloat16)
    bias = edge_bias.reshape(node_count, head_count, fanout)
    high = lax.reduce_precision(bias, 8, 7)
    middle = lax.reduce_precision(bias - high, 8, 7)
    low = bias - high - middle
    live_row = (valid == 1).astype(jnp.float32)[:, None, :]
    filler = jnp.zeros((node_count, 8 - head_count, fanout), jnp.float32)
    live_fill = jnp.concatenate([live_row, filler[:, 1:]], axis=1)
    edge_rows = jnp.concatenate([high, live_fill, middle, filler, low, filler], axis=1)
    group = 16
    dense = pl.pallas_call(
        spread_edges,
        grid=(node_count // group,),
        in_specs=[
            pl.BlockSpec((group, fanout), lambda i: (i, 0)),
            pl.BlockSpec((group, 24, fanout), lambda i: (i, 0, 0)),
        ],
        out_specs=pl.BlockSpec((group, 8, slot_count), lambda i: (i, 0, 0)),
        out_shape=jax.ShapeDtypeStruct((node_count, 8, slot_count), jnp.float32),
        cost_estimate=pl.CostEstimate(
            flops=2 * node_count * 24 * fanout * slot_count,
            bytes_accessed=32 * node_count * slot_count,
            transcendentals=0,
        ),
    )(neighbours, edge_rows.astype(jnp.bfloat16))
    dense = jnp.transpose(dense, (1, 0, 2))
    mesh_wide, mesh_factor, mesh_normed = normalize(mesh_h, gain_mesh)
    queries = (
        jnp.dot(mesh_normed, w_query, preferred_element_type=jnp.float32) * logit_scale
    ).astype(jnp.bfloat16)
    att_grad = jnp.einsum("me,de->md", out_grad, w_out, preferred_element_type=jnp.float32).astype(
        jnp.bfloat16
    )
    by_head = pl.BlockSpec((node_count, head_width), lambda h: (0, h))
    attended_rows, query_gradient, back = pl.pallas_call(
        functools.partial(attend, logit_scale),
        grid=(head_count,),
        in_specs=[
            by_head,
            pl.BlockSpec((slot_count, head_width), lambda h: (0, h)),
            pl.BlockSpec((slot_count, head_width), lambda h: (0, head_count + h)),
            by_head,
            pl.BlockSpec((1, node_count, slot_count), lambda h: (h, 0, 0)),
            pl.BlockSpec((1, node_count, slot_count), lambda h: (head_count, 0, 0)),
        ],
        out_specs=[
            by_head,
            by_head,
            pl.BlockSpec((2, slot_count, head_width), lambda h: (0, 0, h)),
        ],
        out_shape=[
            jax.ShapeDtypeStruct((node_count, model_width), jnp.bfloat16),
            jax.ShapeDtypeStruct((node_count, model_width), jnp.bfloat16),
            jax.ShapeDtypeStruct((2, slot_count, model_width), jnp.bfloat16),
        ],
        cost_estimate=pl.CostEstimate(
            flops=12 * node_count * slot_count * model_width,
            bytes_accessed=8 * slot_count * model_width,
            transcendentals=node_count * head_count * slot_count,
        ),
    )(queries, recv_pair, recv_pair, att_grad, dense, dense)
    mesh_out = (
        mesh_wide + jnp.dot(attended_rows, w_out, preferred_element_type=jnp.float32)
    ).astype(jnp.bfloat16)
    grad_wo = jnp.einsum("md,me->de", attended_rows, out_grad, preferred_element_type=jnp.float32)
    grad_wk = jnp.einsum("sd,se->de", arrived, back[0], preferred_element_type=jnp.float32)
    grad_wv = jnp.einsum("sd,se->de", arrived, back[1], preferred_element_type=jnp.float32)
    grad_wq = jnp.einsum(
        "md,me->de", mesh_normed, query_gradient, preferred_element_type=jnp.float32
    )
    weight_grads = reduce_weights(jnp.stack([grad_wq, grad_wk, grad_wv, grad_wo]))
    back_packet = (
        jnp.concatenate([back[0], back[1]], axis=1)
        .reshape(3, block, 2 * model_width)
    )
    home_pieces = []
    for offset in (0, 1, 2):
        piece = back_packet[offset]
        if offset != 1:
            piece = from_behind(piece, "grid", 1 - offset)
        home_pieces.append(piece)
    home = jnp.stack(home_pieces)
    home = home.reshape(3, sub_count, slots_per, 2 * model_width)
    returned = lax.all_to_all(home, "sub", split_axis=1, concat_axis=1, tiled=True).reshape(
        slot_count, 2 * model_width
    )
    slot_back = jnp.einsum("se,de->sd", returned, w_pair, preferred_element_type=jnp.float32)
    normed_grad = jnp.einsum(
        "sp,sd->pd",
        send_onehot,
        slot_back.astype(jnp.bfloat16),
        preferred_element_type=jnp.float32,
    )
    grid_grad = normalize_back(grid_wide, grid_factor, gain_grid, normed_grad).astype(jnp.bfloat16)
    mesh_normed_grad = jnp.einsum(
        "me,de->md", query_gradient, w_query, preferred_element_type=jnp.float32
    )
    mesh_grad = (
        out_grad.astype(jnp.float32)
        + normalize_back(mesh_wide, mesh_factor, gain_mesh, mesh_normed_grad)
    ).astype(jnp.bfloat16)
    return (mesh_out, mesh_grad, grid_grad, weight_grads)


def solution(mesh):
    in_specs = (
        P(("grid", "sub"), None),
        P(("grid", "sub"), None),
        P(),
        P(),
        P(),
        P(),
        P(),
        P(),
        P(("grid", "sub"), None),
        P(("grid", "sub"), None),
        P(("grid", "sub"), None),
        P(("grid", "sub"), None, None, None),
        P(("grid", "sub"), None),
    )
    out_specs = (P(("grid", "sub"), None), P(("grid", "sub"), None), P(("grid", "sub"), None), P())
    return jax.shard_map(shards, mesh=mesh, in_specs=in_specs, out_specs=out_specs, check_vma=False)
```

profile of v0, /device:TPU:0, one launch (start us, length us, event | category | flops | bytes accessed | tf_op | source)
XLA Modules:
  0.0 268.1 jit_solution(15670856888362652112)
XLA Ops:
  7.2 3.0 %copy.32 = bf16[2048,512]{0,1:T(8,128)(2,1)S(1)} copy(bf16[2048,512]{1,0:T(8,128)(2,1)} %param.13) | data formatting | bytes 4194304 | tf_op args[0]
  11.0 2.0 fusion.14
  13.9 6.3 %all-to-all-start = ((bf16[3,4,64,512]{3,2,0,1:T(8,128)(2,1)}), bf16[3,4,64,512]{3,2,0,1:T(8,128)(2,1)S(1)}, u32[]{:S(2)}, u32[]{:S(2)}) async-start(bf16[3,4,64,512]{3,2,0,1:T(8,128)(2,1)} %copy.33), calls=%async_computation | async-start | bytes 1572864 | tf_op jit(solution)/shard_map/all_to_all | solution.py:108
  20.2 1.7 reshape.77
  23.3 1.7 fusion.21
  26.2 4.9 %concatenate.16.rows_ref = bf16[64,24,96]{2,1,0:T(8,128)(2,1)} concatenate(bf16[64,4,96]{2,1,0:T(4,128)(2,1)} %get-tuple-element.36, bf16[64,1,96]{2,1,0:T(2,128)(2,1)} %copy.34, bf16[64,3,96]{2,1,0:T(4,128)(2,1)} %slice.38, bf16[64,4,96]{2,1,0:T(4,128)(2,1)} %get-tuple-element.35, bf16[64,4,96]{2,1,0:T(4,128)(2,1)} %broadcast_in_dim.9, bf16[64,4,96]{2,1,0:T(4,128)(2,1)} %get-tuple-element.34, ...), dimensions={1} | concatenate | bytes 589824 | tf_op jit(solution)/shard_map/concatenate | solution.py:126
  31.2 1.1 constant_dynamic-update-slice_fusion.1
  35.4 5.0 %all-to-all-done = bf16[3,4,64,512]{3,2,0,1:T(8,128)(2,1)S(1)} async-done(((bf16[3,4,64,512]{3,2,0,1:T(8,128)(2,1)}), bf16[3,4,64,512]{3,2,0,1:T(8,128)(2,1)S(1)}, u32[]{:S(2)}, u32[]{:S(2)}) %all-to-all-start) | async-done | bytes 786464 | tf_op jit(solution)/shard_map/all_to_all | solution.py:108
  41.2 1.3 collective-permute-start.1
  42.6 1.3 collective-permute-start
  43.9 6.4 %shard_map.156 = f32[64,8,768]{2,1,0:T(8,128)} custom-call(s32[64,96]{1,0:T(8,128)} %nbr_ref.1, bf16[64,24,96]{2,1,0:T(8,128)(2,1)} %concatenate.16.rows_ref), custom_call_target="tpu_custom_call" | custom-call | flops 226492416 | bytes 1572864 | tf_op jit(solution)/shard_map/pallas_call | solution.py:128
  50.3 3.2 %copy.42 = f32[64,8,768]{2,0,1:T(8,128)} copy(f32[64,8,768]{2,1,0:T(8,128)} %shard_map.156) | data formatting | bytes 3145728 | tf_op jit(solution)/shard_map/pallas_call | solution.py:128
  54.4 3.1 %convolution_convert_fusion.k_ref.v_ref = bf16[768,1024]{1,0:T(8,128)(2,1)} fusion(bf16[512,1024]{1,0:T(8,128)(2,1)S(1)} %copy-done.7, bf16[256,512]{1,0:T(8,128)(2,1)S(1)} %collective-permute-done.1, bf16[256,512]{1,0:T(8,128)(2,1)S(1)} %bitcast.53, bf16[256,512]{1,0:T(8,128)(2,1)} %collective-permute-done), kind=kOutput, calls=%fused_computation.23 | convolution fusion | flops 808452096 | bytes 3407872 | tf_op jit(solution)/shard_map/dot_general | solution.py:118
  57.5 6.5 %shard_map.157 = (bf16[64,512]{1,0:T(8,128)(2,1)}, bf16[64,512]{1,0:T(8,128)(2,1)}, bf16[2,768,512]{2,1,0:T(8,128)(2,1)}) custom-call(bf16[64,512]{1,0:T(8,128)(2,1)} %fusion.17.q_ref, bf16[768,1024]{1,0:T(8,128)(2,1)} %convolution_convert_fusion.k_ref.v_ref, bf16[768,1024]{1,0:T(8,128)(2,1)} %convolution_convert_fusion.k_ref.v_ref, ...), custom_call_target="tpu_custom_call" | custom-call | flops 301989888 | bytes 3145728 | tf_op jit(solution)/shard_map/pallas_call | solution.py:152
  63.9 1.5 slice_bitcast_fusion.1
  65.6 1.3 collective-permute-start.3
  66.9 5.4 %collective-permute-start.2 = (bf16[256,1024]{1,0:T(8,128)(2,1)S(1)}, bf16[256,1024]{1,0:T(8,128)(2,1)S(1)}, u32[]{:S(2)}, u32[]{:S(2)}) collective-permute-start(bf16[256,1024]{1,0:T(8,128)(2,1)S(1)} %get-tuple-element.26), channel_id=1, source_target_pairs={{0,4},{4,8},{8,12},{12,16},{16,20},{20,24},{24,28},{1,5},{5,9},{9,... | collective-permute-start | bytes 1572872 | tf_op jit(solution)/shard_map/ppermute | solution.py:16
  72.3 1.5 collective-permute-done.2
  73.8 1.3 pad_maximum_fusion.1
  75.1 4.5 %all-to-all-start.1 = ((bf16[3,4,64,1024]{3,2,0,1:T(8,128)(2,1)}), bf16[3,4,64,1024]{3,2,0,1:T(8,128)(2,1)}, u32[]{:S(2)}, u32[]{:S(2)}) async-start(bf16[3,4,64,1024]{3,2,0,1:T(8,128)(2,1)} %pad_maximum_fusion.1), calls=%async_computation.1 | async-start | bytes 3145728 | tf_op jit(solution)/shard_map/all_to_all | solution.py:201
  81.3 1.5 convolution_bitcast_fusion.2
  82.8 1.5 convolution_bitcast_fusion.3
  84.4 2.4 pad_maximum_fusion
  86.8 1.1 fusion.29
  88.0 1.4 fusion.28
  90.3 31.5 %all-to-all-done.1 = bf16[3,4,64,1024]{3,2,0,1:T(8,128)(2,1)} async-done(((bf16[3,4,64,1024]{3,2,0,1:T(8,128)(2,1)}), bf16[3,4,64,1024]{3,2,0,1:T(8,128)(2,1)}, u32[]{:S(2)}, u32[]{:S(2)}) %all-to-all-start.1) | async-done | bytes 1572896 | tf_op jit(solution)/shard_map/all_to_all | solution.py:201
  121.7 2.7 %copy.39 = bf16[3,4,64,1024]{3,2,1,0:T(8,128)(2,1)} copy(bf16[3,4,64,1024]{3,2,0,1:T(8,128)(2,1)} %all-to-all-done.1) | data formatting | bytes 3145728 | tf_op jit(solution)/shard_map/all_to_all | solution.py:201
  124.4 6.9 %fusion.8 = (f32[2048]{0:T(1024)S(1)}, f32[2048,512]{0,1:T(8,128)}) fusion(bf16[2048,512]{0,1:T(8,128)(2,1)S(1)} %copy.32, f32[512]{0:T(512)S(1)} %copy-done.17, bf16[768,1024]{1,0:T(8,128)(2,1)} %bitcast.49, bf16[512,1024]{1,0:T(8,128)(2,1)} %copy-done.6, s32[768]{0:T(1024)S(1)} %copy-done.15), kind=kOutput, calls=%fused_computation.13 | convolution fusion | flops 2422077440 | bytes 8926208 | tf_op jit(solution)/shard_map/sp,sd->pd/dot_general | solution.py:205
  131.3 4.7 %fusion.7 = bf16[2048,512]{0,1:T(8,128)(2,1)} fusion(bf16[2048,512]{0,1:T(8,128)(2,1)S(1)} %copy.32, f32[2048,512]{0,1:T(8,128)} %get-tuple-element.44, f32[2048]{0:T(1024)S(1)} %broadcast_multiply_fusion, f32[2048]{0:T(1024)S(1)} %get-tuple-element.37, f32[512]{0:T(512)S(1)} %copy-done.17, f32[2048]{0:T(1024)S(1)} %get-tuple-element.38), kind=kLoop, calls=%fused_computation.12 | loop fusion | flops 7340032 | bytes 8415232 | tf_op jit(solution)/shard_map/convert_element_type | solution.py:211
  136.0 4.0 %copy.40 = bf16[2048,512]{1,0:T(8,128)(2,1)} copy(bf16[2048,512]{0,1:T(8,128)(2,1)} %fusion.7) | data formatting | bytes 4194304
  140.0 116.6 %all-reduce.2.cloned.1.call-done = f32[4,512,512]{2,1,0:T(8,128)} async-done(((f32[4,512,512]{2,1,0:T(8,128)}), f32[4,512,512]{2,1,0:T(8,128)}) %all-reduce.2.cloned.1.call-update) | async-done | bytes 4194320 | tf_op jit(solution)/shard_map/psum | solution.py:70
  256.6 4.6 %copy.45 = f32[4,512,512]{2,1,0:T(8,128)} copy(f32[4,512,512]{2,1,0:T(8,128)} %all-reduce.2.cloned.1.call-done) | data formatting | bytes 8388608
  (61 shorter events, 12.0 us)
Async XLA Ops:
  7.2 46.3 %copy-start = (bf16[512,512]{1,0:T(8,128)(2,1)S(1)}, bf16[512,512]{1,0:T(8,128)(2,1)}, u32[]{:S(2)}) copy-start(bf16[512,512]{1,0:T(8,128)(2,1)} %param.17) | copy-start | bytes 1572868
  10.2 0.7 copy-start.12
  10.2 0.8 copy-start.16
  10.9 2.0 copy-start.14
  12.9 18.2 %copy-start.1 = (bf16[64,512]{1,0:T(8,128)(2,1)S(1)}, bf16[64,512]{1,0:T(8,128)(2,1)}, u32[]{:S(2)}) copy-start(bf16[64,512]{1,0:T(8,128)(2,1)} %param.14) | copy-start | bytes 196612
  13.9 26.5 %all-to-all-start = ((bf16[3,4,64,512]{3,2,0,1:T(8,128)(2,1)}), bf16[3,4,64,512]{3,2,0,1:T(8,128)(2,1)S(1)}, u32[]{:S(2)}, u32[]{:S(2)}) async-start(bf16[3,4,64,512]{3,2,0,1:T(8,128)(2,1)} %copy.33), calls=%async_computation | async-start | bytes 1572864 | tf_op jit(solution)/shard_map/all_to_all | solution.py:108
  20.2 14.2 %copy-start.5 = (bf16[64,512]{1,0:T(8,128)(2,1)S(1)}, bf16[64,512]{1,0:T(8,128)(2,1)}, u32[]{:S(2)}) copy-start(bf16[64,512]{1,0:T(8,128)(2,1)} %param.25) | copy-start | bytes 196612
  31.1 3.3 %copy-start.2 = (bf16[512,512]{1,0:T(8,128)(2,1)S(1)}, bf16[512,512]{1,0:T(8,128)(2,1)}, u32[]{:S(2)}) copy-start(bf16[512,512]{1,0:T(8,128)(2,1)} %param.20) | copy-start | bytes 1572868
  33.5 1.0 copy-start.6
  41.2 13.1 %collective-permute-start.1 = (bf16[256,512]{1,0:T(8,128)(2,1)}, bf16[256,512]{1,0:T(8,128)(2,1)S(1)}, u32[]{:S(2)}, u32[]{:S(2)}) collective-permute-start(bf16[256,512]{1,0:T(8,128)(2,1)} %bitcast.3), channel_id=1, source_target_pairs={{0,4},{4,8},{8,12},{12,16},{16,20},{20,24},{24,28},{1,5},{5,9},{9,... | collective-permute-start | bytes 786440 | tf_op jit(solution)/shard_map/ppermute | solution.py:16
  42.5 10.9 %copy-start.11 = (f32[512]{0:T(512)S(1)}, f32[512]{0:T(512)}, u32[]{:S(2)}) copy-start(f32[512]{0:T(512)} %param.16) | copy-start | bytes 6148
  42.5 10.9 %copy-start.13 = (f32[64]{0:T(128)S(1)}, f32[64]{0:T(128)}, u32[]{:S(2)}) copy-start(f32[64]{0:T(128)} %get-tuple-element.40) | copy-start | bytes 772
  42.6 11.8 %collective-permute-start = (bf16[256,512]{1,0:T(8,128)(2,1)}, bf16[256,512]{1,0:T(8,128)(2,1)}, u32[]{:S(2)}, u32[]{:S(2)}) collective-permute-start(bf16[256,512]{1,0:T(8,128)(2,1)} %bitcast.1), channel_id=1, source_target_pairs={{4,0},{8,4},{12,8},{16,12},{20,16},{24,20},{28,24},{5,1},{9,5},{13... | collective-permute-start | bytes 786440 | tf_op jit(solution)/shard_map/ppermute | solution.py:16
  50.3 4.1 %copy-start.7 = (bf16[512,1024]{1,0:T(8,128)(2,1)S(1)}, bf16[512,1024]{1,0:T(8,128)(2,1)}, u32[]{:S(2)}) copy-start(bf16[512,1024]{1,0:T(8,128)(2,1)} %copy-done.6) | copy-start | bytes 3145732
  50.3 4.1 %copy-start.8 = (bf16[1,4,64,512]{3,2,0,1:T(8,128)(2,1)S(1)}, bf16[1,4,64,512]{3,2,0,1:T(8,128)(2,1)}, u32[]{:S(2)}) copy-start(bf16[1,4,64,512]{3,2,0,1:T(8,128)(2,1)} %get-tuple-element.33) | copy-start | bytes 786436
  65.6 6.7 %collective-permute-start.3 = (bf16[256,1024]{1,0:T(8,128)(2,1)S(1)}, bf16[256,1024]{1,0:T(8,128)(2,1)S(1)}, u32[]{:S(2)}, u32[]{:S(2)}) collective-permute-start(bf16[256,1024]{1,0:T(8,128)(2,1)S(1)} %get-tuple-element.27), channel_id=1, source_target_pairs={{4,0},{8,4},{12,8},{16,12},{20,16},{24,20},{28,24},{5,1},{9,5},{13... | collective-permute-start | bytes 1572872 | tf_op jit(solution)/shard_map/ppermute | solution.py:16
  66.9 6.9 %collective-permute-start.2 = (bf16[256,1024]{1,0:T(8,128)(2,1)S(1)}, bf16[256,1024]{1,0:T(8,128)(2,1)S(1)}, u32[]{:S(2)}, u32[]{:S(2)}) collective-permute-start(bf16[256,1024]{1,0:T(8,128)(2,1)S(1)} %get-tuple-element.26), channel_id=1, source_target_pairs={{0,4},{4,8},{8,12},{12,16},{16,20},{20,24},{24,28},{1,5},{5,9},{9,... | collective-permute-start | bytes 1572872 | tf_op jit(solution)/shard_map/ppermute | solution.py:16
  75.1 4.8 %copy-start.9 = (bf16[64,512]{1,0:T(8,128)(2,1)S(1)}, bf16[64,512]{1,0:T(8,128)(2,1)}, u32[]{:S(2)}) copy-start(bf16[64,512]{1,0:T(8,128)(2,1)} %get-tuple-element.7) | copy-start | bytes 196612
  75.1 5.1 %copy-start.10 = (bf16[64,512]{1,0:T(8,128)(2,1)S(1)}, bf16[64,512]{1,0:T(8,128)(2,1)}, u32[]{:S(2)}) copy-start(bf16[64,512]{1,0:T(8,128)(2,1)} %get-tuple-element.8) | copy-start | bytes 196612
  75.1 46.6 %all-to-all-start.1 = ((bf16[3,4,64,1024]{3,2,0,1:T(8,128)(2,1)}), bf16[3,4,64,1024]{3,2,0,1:T(8,128)(2,1)}, u32[]{:S(2)}, u32[]{:S(2)}) async-start(bf16[3,4,64,1024]{3,2,0,1:T(8,128)(2,1)} %pad_maximum_fusion.1), calls=%async_computation.1 | async-start | bytes 3145728 | tf_op jit(solution)/shard_map/all_to_all | solution.py:201
  79.6 176.9 %all-reduce.2.cloned.1.call-start = ((), (), s32[]{:S(2)}) async-start(), calls=%async_computation.2 | async-start | bytes 8388608 | tf_op jit(solution)/shard_map/psum | solution.py:70
  79.9 1.4 copy-start.4
  86.8 2.6 copy-start.3
  88.0 36.4 %copy-start.15 = (s32[768]{0:T(1024)S(1)}, s32[768]{0:T(1024)}, u32[]{:S(2)}) copy-start(s32[768]{0:T(1024)} %copy-done.14) | copy-start | bytes 9220
  88.0 36.4 %copy-start.17 = (f32[512]{0:T(512)S(1)}, f32[512]{0:T(512)}, u32[]{:S(2)}) copy-start(f32[512]{0:T(512)} %param.15) | copy-start | bytes 6148
Sparse Core Ops, SparseCore 0:
  87.0 169.5 all-reduce.1
where the time goes:
time: 269 us; the launch traced here: 268 us
  waiting for transfers between devices  155 us (58%)
  local copies, waits for them, and re-layouts  32.8 us (12%)
  starting transfers between devices  20.4 us (8%)
  matrix products  19.5 us (7%)
  between operations  14.3 us (5%)
  other arithmetic  13.7 us (5%)
  Pallas kernels  12.9 us (5%)
    psum x1, waiting for transfers between devices, reduce_weights(): return lax.psum(local_grads, ('grid', 'sub'))  117 us
    all_to_all x1, waiting for transfers between devices, shards(): lax.all_to_all(home, 'sub', split_axis=1, concat_axis=1, tiled=True)  31.5 us
    unnamed x40, local copies, waits for them, and re-layouts  14 us
    ppermute x4, starting transfers between devices, from_behind(): return lax.ppermute(block, axis, route)  9.29 us
    dot_general x1, matrix products, shards(): jnp.einsum('sp,sd->pd', send_onehot, slot_back.astype(jnp.bfloat16), pref...  6.88 us
    pallas_call x1, Pallas kernels, shards(): pl.pallas_call(functools.partial(attend, logit_scale), grid=(head_count,)...  6.45 us
    pallas_call x1, Pallas kernels, shards(): pl.pallas_call(spread_edges, grid=(node_count // group,), in_specs=[pl.Bl...  6.44 us
    all_to_all x1, starting transfers between devices, shards(): lax.all_to_all(packet, 'sub', split_axis=1, concat_axis=1, tiled=True)  6.35 us
  transfers between devices with their start and end apart: 7, of which 4 were waited for; matrix products, arithmetic and copies ran while one was open for 17% of the time, Pallas kernels for 2%

commit v1 on v0

v1 whole, which is shorter than its diff:
```python
import functools

import jax
import jax.numpy as jnp
from jax import lax
from jax.experimental import pallas as pl
from jax.experimental.pallas import tpu as pltpu
from jax.sharding import PartitionSpec as P

EPSILON = 1e-06
NEG_FILL = -1e30
F32 = jnp.float32
BF16 = jnp.bfloat16
NN = (((1,), (0,)), ((), ()))
NT = (((1,), (1,)), ((), ()))
TN = (((0,), (0,)), ((), ()))
LANES = 128
ROWS = 24


def dot(a, b, dims=NN):
    return lax.dot_general(a, b, dims, preferred_element_type=F32)


def normalize(values_in, gain_row):
    widened = values_in.astype(F32)
    factor = lax.rsqrt(jnp.mean(widened * widened, axis=-1, keepdims=True) + EPSILON)
    return (widened, factor, (widened * factor * gain_row).astype(BF16))


def normalize_back(widened, factor, gain_row, upstream):
    scaled = gain_row * upstream
    inner_mean = jnp.mean(widened * scaled, axis=-1, keepdims=True)
    return factor * scaled - widened * factor**3 * inner_mean


def layer(
    n_grid,
    n_sub,
    grid_x, mesh_h, gain_g, gain_m, w_q, w_k, w_v, w_o, bias, nbr, valid, rows, out_grad,
    returned_out, gathered, mesh_out, mesh_grad,
    x_s, mesh_s, gg_s, gm_s, wq_s, wk_s, wv_s, wo_s, bias_s, nbr_s, valid_s, rows_s, og_s,
    packet, arrived, slot_back, returned,
    edge_rows, dense, slot_of, q_s, ag_s, mn_s, k_s, v_s, att_s, qg_s, back_k, back_v, mo_s, mg_s,
    part, core_out, core_in, chip_acc, chip_out, chip_in, sub_acc, sub_out, sub_in, whole,
    load_sem, fwd_send, fwd_recv, back_send, back_recv,
    core_send, core_recv, chip_send, chip_recv, sub_send, sub_recv,
    subg_send, subg_recv, chipg_send, chipg_recv, coreg_send, coreg_recv, store_sem,
):
    g = lax.axis_index("grid")
    c = lax.axis_index("sub")
    core = lax.rem(g, 2)
    chip = lax.div(g, 2)
    chips = n_grid // 2
    other_core = g + 1 - 2 * core
    points, width = x_s.shape
    nodes = mesh_s.shape[0]
    slots_per = rows_s.shape[3]
    fanout = nbr_s.shape[1]
    heads = bias_s.shape[1] // fanout
    head = width // heads
    slots = 3 * n_sub * slots_per
    scale = head ** (-0.5)
    half = points // 2

    loads = {}
    pairs = (
        ("rows", rows, rows_s), ("x", grid_x, x_s), ("gg", gain_g, gg_s), ("nbr", nbr, nbr_s),
        ("bias", bias, bias_s), ("valid", valid, valid_s), ("mesh", mesh_h, mesh_s),
        ("gm", gain_m, gm_s), ("wq", w_q, wq_s), ("og", out_grad, og_s), ("wo", w_o, wo_s),
        ("wk", w_k, wk_s), ("wv", w_v, wv_s),
    )
    for at, (name, source, target) in enumerate(pairs):
        loads[name] = pltpu.make_async_copy(source, target, load_sem.at[at])
        loads[name].start()

    def wrap(value, size):
        return lax.rem(value + size, size)

    def remote(source, target, send, recv, to_grid, to_sub):
        return pltpu.make_async_remote_copy(
            src_ref=source, dst_ref=target, send_sem=send, recv_sem=recv,
            device_id={"grid": to_grid, "sub": to_sub}, device_id_type=pl.DeviceIdType.MESH,
        )

    barrier = pltpu.get_barrier_semaphore()
    peers = [
        (wrap(g + o, n_grid), wrap(c + k, n_sub))
        for k in range(n_sub) for o in (-1, 0, 1) if (o, k) != (0, 0)
    ] + [(lax.rem(chip + j, chips) * 2 + core, c) for j in range(1, chips)]
    for to_grid, to_sub in peers:
        pl.semaphore_signal(
            barrier, inc=1, device_id={"grid": to_grid, "sub": to_sub},
            device_id_type=pl.DeviceIdType.MESH,
        )

    far_first = sorted(range(n_sub), key=lambda k: -min(k, n_sub - k))

    loads["rows"].wait()
    eye = (
        lax.broadcasted_iota(jnp.int32, (slots_per, slots_per), 0)
        == lax.broadcasted_iota(jnp.int32, (slots_per, slots_per), 1)
    )
    pl.semaphore_wait(barrier, len(peers))
    forward = {}
    for o in (0, 2, 1):
        low, span = (0, half) if o == 0 else (half, points - half) if o == 2 else (0, points)
        lane = lax.broadcasted_iota(jnp.int32, (slots_per, span), 1) + low
        picks = []
        for s in range(n_sub):
            row = rows_s[0, o, pl.ds(s, 1), :].astype(F32)
            column = jnp.sum(jnp.where(eye, row, 0.0), axis=1, keepdims=True).astype(jnp.int32)
            picks.append(jnp.where(lane == column, 1.0, 0.0).astype(BF16))
        onehot = jnp.concatenate(picks, axis=0)
        if o == 0:
            loads["x"].wait()
            loads["gg"].wait()
        chosen = dot(onehot, x_s[pl.ds(low, span), :])
        factor = lax.rsqrt(jnp.mean(chosen * chosen, axis=-1, keepdims=True) + EPSILON)
        packet[o] = (chosen * factor * gg_s[...]).astype(BF16).reshape(n_sub, slots_per, width)
        for k in far_first:
            if (o, k) == (1, 0):
                continue
            to_sub = lax.rem(c + k, n_sub)
            forward[o, k] = remote(
                packet.at[o, to_sub], arrived.at[k, o],
                fwd_send.at[o * n_sub + k], fwd_recv.at[o * n_sub + k],
                wrap(g + o - 1, n_grid), to_sub,
            )
            forward[o, k].start()
    arrived[0, 1] = packet[1, c]

    for name in ("nbr", "bias", "valid"):
        loads[name].wait()
    named = nbr_s[...]
    offset_of = lax.div(named, n_sub * slots_per)
    sub_of = lax.rem(lax.div(named, slots_per), n_sub)
    turn = lax.rem(c - sub_of + n_sub, n_sub)
    slot_of[...] = (turn * 3 + offset_of) * slots_per + lax.rem(named, slots_per)
    edge_rows[...] = jnp.zeros(edge_rows.shape, F32)
    for h in range(heads):
        values = bias_s[:, h * fanout:(h + 1) * fanout]
        high = values.astype(BF16).astype(F32)
        middle = (values - high).astype(BF16).astype(F32)
        edge_rows[pl.ds(h, nodes, stride=ROWS), :fanout] = high
        edge_rows[pl.ds(8 + h, nodes, stride=ROWS), :fanout] = middle
        edge_rows[pl.ds(16 + h, nodes, stride=ROWS), :fanout] = values - high - middle
    edge_rows[pl.ds(heads, nodes, stride=ROWS), :fanout] = jnp.where(valid_s[...] == 1, 1.0, 0.0)

    slot_ids = lax.broadcasted_iota(jnp.int32, (slots, fanout), 0)
    group = 8

    def spread(step, carry):
        for inner in range(group):
            node = step * group + inner
            names = slot_ids == slot_of[pl.ds(node, 1), :]
            onehot = jnp.where(names, 1.0, 0.0).astype(BF16)
            at = pl.multiple_of(node * ROWS, 8)
            spread_rows = dot(edge_rows[pl.ds(at, ROWS), :fanout].astype(BF16), onehot, NT)
            total = (spread_rows[16:24] + spread_rows[8:16]) + spread_rows[:8]
            for tile in range(slots // LANES):
                dense[tile, pl.ds(pl.multiple_of(node * 8, 8), 8), :] = (
                    total[:, tile * LANES:(tile + 1) * LANES]
                )
        return carry

    lax.fori_loop(0, nodes // group, spread, 0)

    for name in ("mesh", "gm", "wq", "og", "wo", "wk", "wv"):
        loads[name].wait()
    mesh_wide, mesh_factor, mesh_normed = normalize(mesh_s[...], gm_s[...])
    mn_s[...] = mesh_normed
    q_s[...] = (dot(mesh_normed, wq_s[...]) * scale).astype(BF16)
    ag_s[...] = dot(og_s[...], wo_s[...], NT).astype(BF16)

    for move in forward.values():
        move.wait_recv()
    rows_in = arrived[...].reshape(slots, width)
    k_s[...] = dot(rows_in, wk_s[...]).astype(BF16)
    v_s[...] = dot(rows_in, wv_s[...]).astype(BF16)

    def spread_of(row):
        return jnp.concatenate(
            [dense[tile, pl.ds(row, nodes, stride=8), :] for tile in range(slots // LANES)], axis=1
        )

    live = spread_of(heads) > 0.5
    for h in range(heads):
        mine = slice(h * head, (h + 1) * head)
        queries, keys, values, att_grad = q_s[:, mine], k_s[:, mine], v_s[:, mine], ag_s[:, mine]
        scores = dot(queries, keys, NT) + spread_of(h)
        peak = jnp.max(jnp.where(live, scores, NEG_FILL), axis=1, keepdims=True)
        terms = jnp.exp(jnp.where(live, scores - peak, NEG_FILL))
        probs = terms / jnp.sum(terms, axis=1, keepdims=True)
        probs_b = probs.astype(BF16)
        att_s[:, mine] = dot(probs_b, values).astype(BF16)
        prob_grads = dot(att_grad, values, NT)
        score_grads = (
            probs * (prob_grads - jnp.sum(probs * prob_grads, axis=1, keepdims=True))
        ).astype(BF16)
        qg_s[:, mine] = (dot(score_grads, keys) * scale).astype(BF16)
        back_k[:, mine] = dot(score_grads, queries, TN).astype(BF16)
        back_v[:, mine] = dot(probs_b, att_grad, TN).astype(BF16)

    backward = {}
    turn_rows = 3 * slots_per
    for k in far_first:
        here = slice(k * turn_rows, (k + 1) * turn_rows)
        total = dot(back_k[here, :], wk_s[...], NT) + dot(back_v[here, :], wv_s[...], NT)
        slot_back[k] = total.astype(BF16).reshape(3, slots_per, width)
        for o in range(3):
            if (o, k) == (1, 0):
                continue
            backward[o, k] = remote(
                slot_back.at[k, o], returned.at[o, c],
                back_send.at[o * n_sub + k], back_recv.at[o * n_sub + k],
                wrap(g + 1 - o, n_grid), wrap(c - k, n_sub),
            )
            backward[o, k].start()
    returned[1, pl.ds(c, 1)] = slot_back[0, 1][None]

    half_rows = width // 2
    chunks = part.shape[0]
    block = half_rows // chips
    moves = {}

    def core_stage(ch, first, second):
        for m, grad in enumerate((first, second)):
            part[ch, m] = grad.reshape(2, half_rows, width)
            core_out[ch, m] = part[ch, m, 1 - core].astype(BF16)
        move = remote(
            core_out.at[ch], core_in.at[ch], core_send.at[ch], core_recv.at[ch], other_core, c
        )
        move.start()
        moves["core", ch] = [move]

    def chip_stage(ch):
        moves["core", ch][0].wait_recv()
        for j in range(chips):
            for m in range(2):
                at = pl.ds(j * block, block)
                total = part[ch, m, core, at, :] + core_in[ch, m, at, :].astype(F32)
                chip_acc[ch, j, m] = total
                chip_out[ch, j, m] = total.astype(BF16)
        moves["chip", ch] = []
        for j in range(1, chips):
            to_chip = lax.rem(chip + j, chips)
            move = remote(
                chip_out.at[ch, to_chip], chip_in.at[ch, j],
                chip_send.at[ch, j], chip_recv.at[ch, j], to_chip * 2 + core, c,
            )
            move.start()
            moves["chip", ch].append(move)

    def sub_stage(ch):
        for move in moves["chip", ch]:
            move.wait_recv()
        for m in range(2):
            total = chip_acc[ch, chip, m]
            for j in range(1, chips):
                total = total + chip_in[ch, j, m].astype(F32)
            for z in range(n_sub):
                piece = total[:, z * (width // n_sub):(z + 1) * (width // n_sub)]
                sub_acc[ch, z, m] = piece
                sub_out[ch, z, m] = piece.astype(BF16)
        moves["sub", ch] = []
        for k in far_first[:-1]:
            to_sub = lax.rem(c + k, n_sub)
            move = remote(
                sub_out.at[ch, to_sub], sub_in.at[ch, k],
                sub_send.at[ch, k], sub_recv.at[ch, k], g, to_sub,
            )
            move.start()
            moves["sub", ch].append(move)

    def sub_gather(ch):
        for move in moves["sub", ch]:
            move.wait_recv()
        total = sub_acc[ch, c]
        for k in range(1, n_sub):
            total = total + sub_in[ch, k].astype(F32)
        whole[ch, chip, pl.ds(c, 1)] = total.astype(BF16)[None]
        moves["subg", ch] = []
        for k in far_first[:-1]:
            move = remote(
                whole.at[ch, chip, c], whole.at[ch, chip, c],
                subg_send.at[ch, k], subg_recv.at[ch, k], g, lax.rem(c + k, n_sub),
            )
            move.start()
            moves["subg", ch].append(move)

    def chip_gather(ch):
        for move in moves["subg", ch]:
            move.wait_recv()
        moves["chipg", ch] = []
        for j in range(1, chips):
            move = remote(
                whole.at[ch, chip], whole.at[ch, chip],
                chipg_send.at[ch, j], chipg_recv.at[ch, j],
                lax.rem(chip + j, chips) * 2 + core, c,
            )
            move.start()
            moves["chipg", ch].append(move)

    def core_gather(ch):
        for move in moves["chipg", ch]:
            move.wait_recv()
        move = remote(
            whole.at[ch], gathered.at[ch, core], coreg_send.at[ch], coreg_recv.at[ch],
            other_core, c,
        )
        move.start()
        moves["coreg", ch] = [move]
        own = pltpu.make_async_copy(whole.at[ch], gathered.at[ch, core], store_sem.at[ch])
        own.start()
        stores.append(own)

    stores = []
    core_stage(0, dot(mn_s[...], qg_s[...], TN), dot(att_s[...], og_s[...], TN))
    core_stage(1, dot(rows_in, back_k[...], TN), dot(rows_in, back_v[...], TN))
    for ch in range(chunks):
        chip_stage(ch)

    mo_s[...] = (mesh_wide + dot(att_s[...], wo_s[...])).astype(BF16)
    mesh_normed_grad = dot(qg_s[...], wq_s[...], NT)
    mg_s[...] = (
        og_s[...].astype(F32)
        + normalize_back(mesh_wide, mesh_factor, gm_s[...], mesh_normed_grad)
    ).astype(BF16)
    for at, (source, target) in enumerate(((mo_s, mesh_out), (mg_s, mesh_grad))):
        own = pltpu.make_async_copy(source, target, store_sem.at[chunks + at])
        own.start()
        stores.append(own)

    for ch in range(chunks):
        sub_stage(ch)
    for ch in range(chunks):
        sub_gather(ch)
    for ch in range(chunks):
        chip_gather(ch)
    for move in backward.values():
        move.wait_recv()
    own = pltpu.make_async_copy(returned, returned_out, store_sem.at[chunks + 2])
    own.start()
    stores.append(own)
    for ch in range(chunks):
        core_gather(ch)
    for ch in range(chunks):
        moves["coreg", ch][0].wait_recv()
    for own in stores:
        own.wait()
    for move in [*forward.values(), *backward.values()] + sum(moves.values(), []):
        move.wait_send()


def finish(
    returned, gathered, mesh_out_in, mesh_grad_in, grid_x, gain_g, rows,
    mesh_out, mesh_grad, grid_grad, weight_grads,
    returned_s, gathered_s, mo_s, mg_s, x_s, gg_s, rows_s, flat, gx_s, w_s, load_sem, store_sem,
):
    points, width = x_s.shape
    n_sub, slots_per = rows_s.shape[2:]
    block = n_sub * slots_per
    chunks, _, chips, _, mats, part_rows, part_lanes = gathered_s.shape
    pieces = x_s.shape[0] // 4
    loads = {}
    pairs = [
        ("rows", rows, rows_s), ("gg", gain_g, gg_s), ("back", returned, returned_s),
    ] + [
        (("x", b), grid_x.at[pl.ds(b * pieces, pieces)], x_s.at[pl.ds(b * pieces, pieces)])
        for b in range(4)
    ] + [
        (("w", ch), gathered.at[ch], gathered_s.at[ch]) for ch in range(chunks)
    ] + [("mo", mesh_out_in, mo_s), ("mg", mesh_grad_in, mg_s)]
    for at, (name, source, target) in enumerate(pairs):
        loads[name] = pltpu.make_async_copy(source, target, load_sem.at[at])
        loads[name].start()
    stores = []

    def store(source, target):
        move = pltpu.make_async_copy(source, target, store_sem.at[len(stores)])
        move.start()
        stores.append(move)

    loads["rows"].wait()
    for o in range(3):
        for s in range(n_sub):
            at = o * block + s * slots_per
            flat[:, at:at + slots_per] = rows_s[0, o, pl.ds(s, 1), :]
    loads["gg"].wait()
    loads["back"].wait()
    back = returned_s[...].reshape(3 * block, width)
    for b in range(4):
        loads["x", b].wait()
        at = slice(b * pieces, (b + 1) * pieces)
        low = 0 if b < 2 else block
        point = lax.broadcasted_iota(jnp.int32, (pieces, 2 * block), 0) + b * pieces
        onehot = jnp.where(point == flat[:, low:low + 2 * block], 1.0, 0.0).astype(BF16)
        normed_grad = dot(onehot, back[low:low + 2 * block])
        wide = x_s[at, :].astype(F32)
        factor = lax.rsqrt(jnp.mean(wide * wide, axis=-1, keepdims=True) + EPSILON)
        gx_s[at, :] = normalize_back(wide, factor, gg_s[...], normed_grad).astype(BF16)
        store(gx_s.at[pl.ds(b * pieces, pieces)], grid_grad.at[pl.ds(b * pieces, pieces)])
    loads["mo"].wait()
    store(mo_s, mesh_out)
    loads["mg"].wait()
    store(mg_s, mesh_grad)
    half_rows = width // 2
    for ch, order in enumerate(((0, 3), (1, 2))):
        loads["w", ch].wait()
        for m, matrix in enumerate(order):
            for core in range(2):
                for j in range(chips):
                    at = core * half_rows + j * part_rows
                    for z in range(n_sub):
                        w_s[matrix, at:at + part_rows, z * part_lanes:(z + 1) * part_lanes] = (
                            gathered_s[ch, core, j, z, m].astype(F32)
                        )
            store(w_s.at[matrix], weight_grads.at[matrix])
    for move in stores:
        move.wait()


def shards(
    n_grid, n_sub,
    grid_x, mesh_h, gain_grid, gain_mesh, w_query, w_key, w_value, w_out,
    edge_bias, neighbours, valid, send_rows, out_grad,
):
    points, width = grid_x.shape
    nodes = mesh_h.shape[0]
    slots_per = send_rows.shape[3]
    fanout = neighbours.shape[1]
    slots = 3 * n_sub * slots_per
    chips = n_grid // 2
    chunks, mats = 2, 2
    half_rows = width // 2
    block, lanes = half_rows // chips, width // n_sub
    anywhere = pl.BlockSpec(memory_space=pl.ANY)
    dma = pltpu.SemaphoreType.DMA
    gain_grid, gain_mesh = gain_grid.reshape(1, width), gain_mesh.reshape(1, width)
    operands = (
        grid_x, mesh_h, gain_grid, gain_mesh, w_query, w_key, w_value, w_out,
        edge_bias, neighbours, valid, send_rows, out_grad,
    )
    blocks = (3, n_sub, slots_per, width)
    turns = (n_sub, 3, slots_per, width)
    node_rows = pltpu.VMEM((nodes, width), BF16)
    slot_rows = pltpu.VMEM((slots, width), BF16)
    piece = (chunks, n_sub, mats, block, lanes)
    returned, gathered, mesh_out, mesh_grad = pl.pallas_call(
        functools.partial(layer, n_grid, n_sub),
        in_specs=[anywhere] * len(operands),
        out_specs=[anywhere] * 4,
        out_shape=[
            jax.ShapeDtypeStruct(blocks, BF16),
            jax.ShapeDtypeStruct((chunks, 2, chips, n_sub, mats, block, lanes), BF16),
            jax.ShapeDtypeStruct((nodes, width), BF16),
            jax.ShapeDtypeStruct((nodes, width), BF16),
        ],
        scratch_shapes=[pltpu.VMEM(a.shape, a.dtype) for a in operands] + [
            pltpu.VMEM(blocks, BF16), pltpu.VMEM(turns, BF16),
            pltpu.VMEM(turns, BF16), pltpu.VMEM(blocks, BF16),
            pltpu.VMEM((nodes * ROWS, LANES), F32),
            pltpu.VMEM((slots // LANES, nodes * 8, LANES), F32),
            pltpu.VMEM((nodes, fanout), jnp.int32),
            node_rows, node_rows, node_rows, slot_rows, slot_rows, node_rows, node_rows,
            slot_rows, slot_rows, node_rows, node_rows,
            pltpu.VMEM((chunks, mats, 2, half_rows, width), F32),
            pltpu.VMEM((chunks, mats, half_rows, width), BF16),
            pltpu.VMEM((chunks, mats, half_rows, width), BF16),
            pltpu.VMEM((chunks, chips, mats, block, width), F32),
            pltpu.VMEM((chunks, chips, mats, block, width), BF16),
            pltpu.VMEM((chunks, chips, mats, block, width), BF16),
            pltpu.VMEM(piece, F32), pltpu.VMEM(piece, BF16), pltpu.VMEM(piece, BF16),
            pltpu.VMEM((chunks, chips, n_sub, mats, block, lanes), BF16),
            dma((len(operands),)),
            dma((3 * n_sub,)), dma((3 * n_sub,)), dma((3 * n_sub,)), dma((3 * n_sub,)),
            dma((chunks,)), dma((chunks,)),
            dma((chunks, chips)), dma((chunks, chips)),
            dma((chunks, n_sub)), dma((chunks, n_sub)),
            dma((chunks, n_sub)), dma((chunks, n_sub)),
            dma((chunks, chips)), dma((chunks, chips)),
            dma((chunks,)), dma((chunks,)),
            dma((chunks + 3,)),
        ],
        compiler_params=pltpu.CompilerParams(collective_id=0, has_side_effects=True),
        name="layer",
    )(*operands)
    return pl.pallas_call(
        finish,
        in_specs=[anywhere] * 7,
        out_specs=[anywhere] * 4,
        out_shape=[
            jax.ShapeDtypeStruct((nodes, width), BF16),
            jax.ShapeDtypeStruct((nodes, width), BF16),
            jax.ShapeDtypeStruct((points, width), BF16),
            jax.ShapeDtypeStruct((chunks * mats, width, width), F32),
        ],
        scratch_shapes=[
            pltpu.VMEM(blocks, BF16),
            pltpu.VMEM((chunks, 2, chips, n_sub, mats, block, lanes), BF16),
            node_rows, node_rows,
            pltpu.VMEM((points, width), BF16), pltpu.VMEM((1, width), F32),
            pltpu.VMEM(send_rows.shape, jnp.int32), pltpu.VMEM((1, slots), jnp.int32),
            pltpu.VMEM((points, width), BF16),
            pltpu.VMEM((chunks * mats, width, width), F32),
            dma((9 + chunks,)), dma((6 + chunks * mats,)),
        ],
        name="finish",
    )(returned, gathered, mesh_out, mesh_grad, grid_x, gain_grid, send_rows)


def solution(mesh):
    by_device = P(("grid", "sub"), None)
    in_specs = (
        by_device, by_device, P(), P(), P(), P(), P(), P(), by_device, by_device, by_device,
        P(("grid", "sub"), None, None, None), by_device,
    )
    out_specs = (by_device, by_device, by_device, P())
    body = functools.partial(shards, mesh.shape["grid"], mesh.shape["sub"])
    return jax.shard_map(body, mesh=mesh, in_specs=in_specs, out_specs=out_specs, check_vma=False)
```

time: 269 us -> 81.7 us (0.30)
  waiting for transfers between devices: 155 us -> 0 us
  Pallas kernels: 12.9 us -> 80.8 us
  local copies, waits for them, and re-layouts: 32.8 us -> 0 us
  starting transfers between devices: 20.4 us -> 0 us
  matrix products: 19.5 us -> 0 us
  other arithmetic: 13.7 us -> 0 us
  between operations: 14.3 us -> 0.64 us
    psum x1 -> x0, waiting for transfers between devices: 117 us -> none  [reduce_weights(): return lax.psum(local_grads, ('grid', 'sub'))]
    pallas_call x2, Pallas kernels: 12.9 us -> 80.8 us  [the longest x1 74.6 us: shards(): pl.pallas_call(functools.partial(layer, n_grid, n_sub), in_specs=[anywher...]
    all_to_all x2 -> x0, waiting for transfers between devices: 36.4 us -> none  [the longest x1 31.5 us: shards(): lax.all_to_all(home, 'sub', split_axis=1, concat_axis=1, tiled=True)]
    dot_general x11 -> x0, matrix products: 19.5 us -> none  [the longest x1 6.88 us: shards(): jnp.einsum('sp,sd->pd', send_onehot, slot_back.astype(jnp.bfloat16), pref...]
    unnamed x40 -> x0, local copies, waits for them, and re-layouts: 14 us -> none
    all_to_all x2 -> x0, starting transfers between devices: 10.9 us -> none  [the longest x1 6.35 us: shards(): lax.all_to_all(packet, 'sub', split_axis=1, concat_axis=1, tiled=True)]
    ppermute x4 -> x0, starting transfers between devices: 9.29 us -> none  [from_behind(): return lax.ppermute(block, axis, route)]
    another operation x4 -> x0, other arithmetic: 6.17 us -> none  [the longest x1 2.44 us: shards(): jnp.stack([grad_wq, grad_wk, grad_wv, grad_wo])]
  transfers between devices with their start and end apart: 7 -> 0, of which waited for: 4 -> 0; matrix products, arithmetic and copies ran while one was open for 17% -> 0% of each run, Pallas kernels for 2% -> 0%
where the time goes in v1:
time: 81.7 us; the launch traced here: 81.4 us
  Pallas kernels  80.8 us (99%)
    pallas_call x1, Pallas kernels, shards(): pl.pallas_call(functools.partial(layer, n_grid, n_sub), in_specs=[anywher...  74.6 us
    pallas_call x1, Pallas kernels, shards(): pl.pallas_call(finish, in_specs=[anywhere] * 7, out_specs=[anywhere] * 4,...  6.13 us

profile of v1, /device:TPU:0, one launch (start us, length us, event | category | flops | bytes accessed | tf_op | source)
XLA Modules:
  0.0 81.4 jit_solution(745355027114350568)
XLA Ops:
  0.6 74.6 %layer.1 = (bf16[3,4,64,512]{3,2,1,0:T(8,128)(2,1)}, bf16[2,2,4,4,2,64,128]{6,5,4,3,2,1,0:T(8,128)(2,1)}, bf16[64,512]{1,0:T(8,128)(2,1)}, bf16[64,512]{1,0:T(8,128)(2,1)}) custom-call(bf16[2048,512]{1,0:T(8,128)(2,1)} %grid_x.3, bf16[64,512]{1,0:T(8,128)(2,1)} %mesh_h.1, f32[1,512]{1,0:T(1,128)} %bitcast.2, f32[1,512]{1,0:T(1,128)} %bitcast.4, ...), custom_call_target="tpu_custom_call" | custom-call | tf_op jit(solution)/shard_map/layer/pallas_call | solution.py:450
  75.3 6.1 %finish.1 = (bf16[64,512]{1,0:T(8,128)(2,1)}, bf16[64,512]{1,0:T(8,128)(2,1)}, bf16[2048,512]{1,0:T(8,128)(2,1)}, f32[4,512,512]{2,1,0:T(8,128)}) custom-call(bf16[3,4,64,512]{3,2,1,0:T(8,128)(2,1)} %get-tuple-element.8.returned, bf16[2,2,4,4,2,64,128]{6,5,4,3,2,1,0:T(8,128)(2,1)} %get-tuple-element.9.gathered, ...), custom_call_target="tpu_custom_call" | custom-call | tf_op jit(solution)/shard_map/finish/pallas_call | solution.py:489

commit v2 on v1

--- a/solution.py
+++ b/solution.py
@@ -41,10 +41,11 @@
     returned_out, gathered, mesh_out, mesh_grad,
     x_s, mesh_s, gg_s, gm_s, wq_s, wk_s, wv_s, wo_s, bias_s, nbr_s, valid_s, rows_s, og_s,
     packet, arrived, slot_back, returned,
-    edge_rows, dense, slot_of, q_s, ag_s, mn_s, k_s, v_s, att_s, qg_s, back_k, back_v, mo_s, mg_s,
+    edge_rows, dense, slot_of, q_s, ag_s, k_s, v_s, att_s, qg_s, back_k, back_v, mo_s, mg_s,
+    known, factor_send, factor_in, factor_part, factor_out_s, factor_core,
     part, core_out, core_in, chip_acc, chip_out, chip_in, sub_acc, sub_out, sub_in, whole,
     load_sem, fwd_send, fwd_recv, back_send, back_recv,
-    core_send, core_recv, chip_send, chip_recv, sub_send, sub_recv,
+    known_send, known_recv, factor_ssem, factor_rsem, core_send, core_recv, chip_send, chip_recv, sub_send, sub_recv,
     subg_send, subg_recv, chipg_send, chipg_recv, coreg_send, coreg_recv, store_sem,
 ):
     g = lax.axis_index("grid")
@@ -101,7 +102,6 @@
         lax.broadcasted_iota(jnp.int32, (slots_per, slots_per), 0)
         == lax.broadcasted_iota(jnp.int32, (slots_per, slots_per), 1)
     )
-    pl.semaphore_wait(barrier, len(peers))
     forward = {}
     for o in (0, 2, 1):
         low, span = (0, half) if o == 0 else (half, points - half) if o == 2 else (0, points)
@@ -118,6 +118,8 @@
         chosen = dot(onehot, x_s[pl.ds(low, span), :])
         factor = lax.rsqrt(jnp.mean(chosen * chosen, axis=-1, keepdims=True) + EPSILON)
         packet[o] = (chosen * factor * gg_s[...]).astype(BF16).reshape(n_sub, slots_per, width)
+        if o == 0:
+            pl.semaphore_wait(barrier, len(peers))
         for k in far_first:
             if (o, k) == (1, 0):
                 continue
@@ -129,6 +131,23 @@
             )
             forward[o, k].start()
     arrived[0, 1] = packet[1, c]
+
+    for name in ("mesh", "gm", "og"):
+        loads[name].wait()
+    mesh_wide, mesh_factor, mesh_normed = normalize(mesh_s[...], gm_s[...])
+    known[0, pl.ds(chip, 1)] = og_s[...][None]
+    known[1, pl.ds(chip, 1)] = mesh_normed[None]
+    known_moves = {}
+    for ch in range(2):
+        known_moves["known", ch] = []
+        for j in range(1, chips):
+            to_chip = lax.rem(chip + j, chips)
+            move = remote(
+                known.at[ch, chip], known.at[ch, chip], known_send.at[ch, j], known_recv.at[ch, j],
+                to_chip * 2 + core, c,
+            )
+            move.start()
+            known_moves["known", ch].append(move)
 
     for name in ("nbr", "bias", "valid"):
         loads[name].wait()
@@ -166,10 +185,8 @@
 
     lax.fori_loop(0, nodes // group, spread, 0)
 
-    for name in ("mesh", "gm", "wq", "og", "wo", "wk", "wv"):
+    for name in ("wq", "wo", "wk", "wv"):
         loads[name].wait()
-    mesh_wide, mesh_factor, mesh_normed = normalize(mesh_s[...], gm_s[...])
-    mn_s[...] = mesh_normed
     q_s[...] = (dot(mesh_normed, wq_s[...]) * scale).astype(BF16)
     ag_s[...] = dot(og_s[...], wo_s[...], NT).astype(BF16)
 
@@ -204,123 +221,222 @@
 
     backward = {}
     turn_rows = 3 * slots_per
-    for k in far_first:
+
+    def turn_back(k):
         here = slice(k * turn_rows, (k + 1) * turn_rows)
         total = dot(back_k[here, :], wk_s[...], NT) + dot(back_v[here, :], wv_s[...], NT)
         slot_back[k] = total.astype(BF16).reshape(3, slots_per, width)
-        for o in range(3):
-            if (o, k) == (1, 0):
-                continue
-            backward[o, k] = remote(
-                slot_back.at[k, o], returned.at[o, c],
-                back_send.at[o * n_sub + k], back_recv.at[o * n_sub + k],
-                wrap(g + 1 - o, n_grid), wrap(c - k, n_sub),
-            )
-            backward[o, k].start()
-    returned[1, pl.ds(c, 1)] = slot_back[0, 1][None]
+
+    def send_home(k, o):
+        backward[o, k] = remote(
+            slot_back.at[k, o], returned.at[o, c],
+            back_send.at[o * n_sub + k], back_recv.at[o * n_sub + k],
+            wrap(g + 1 - o, n_grid), wrap(c - k, n_sub),
+        )
+        backward[o, k].start()
 
     half_rows = width // 2
-    chunks = part.shape[0]
+    chunks = whole.shape[0]
     block = half_rows // chips
+    lanes = width // n_sub
+    chip_bits, sub_bits = chips.bit_length() - 1, n_sub.bit_length() - 1
     moves = {}
-
-    def core_stage(ch, first, second):
-        for m, grad in enumerate((first, second)):
-            part[ch, m] = grad.reshape(2, half_rows, width)
-            core_out[ch, m] = part[ch, m, 1 - core].astype(BF16)
-        move = remote(
-            core_out.at[ch], core_in.at[ch], core_send.at[ch], core_recv.at[ch], other_core, c
-        )
-        move.start()
-        moves["core", ch] = [move]
-
-    def chip_stage(ch):
-        moves["core", ch][0].wait_recv()
+    stores = []
+
+    def flip(index, bit):
+        return index + bit - 2 * bit * lax.rem(lax.div(index, bit), 2)
+
+    def reverse(index, bits):
+        total = 0
+        for t in range(bits):
+            total = total + lax.rem(lax.div(index, 2**t), 2) * 2 ** (bits - 1 - t)
+        return total
+
+    chip_of = (chip, reverse(chip, chip_bits))
+    part_of = lax.rem(c, 2)
+
+    def start(key, *move):
+        moves.setdefault(key, []).append(remote(*move))
+        moves[key][-1].start()
+
+    def arrive(key):
+        for move in moves[key]:
+            move.wait_recv()
+
+    def factor_out(ch):
+        source = (att_s, qg_s)[ch]
+        piece = width // chips
         for j in range(chips):
-            for m in range(2):
-                at = pl.ds(j * block, block)
-                total = part[ch, m, core, at, :] + core_in[ch, m, at, :].astype(F32)
-                chip_acc[ch, j, m] = total
-                chip_out[ch, j, m] = total.astype(BF16)
-        moves["chip", ch] = []
+            factor_send[ch, j] = source[:, j * piece:(j + 1) * piece]
         for j in range(1, chips):
             to_chip = lax.rem(chip + j, chips)
-            move = remote(
-                chip_out.at[ch, to_chip], chip_in.at[ch, j],
-                chip_send.at[ch, j], chip_recv.at[ch, j], to_chip * 2 + core, c,
+            start(
+                ("factor", ch), factor_send.at[ch, to_chip], factor_in.at[ch, chip],
+                factor_ssem.at[ch, j], factor_rsem.at[ch, j], to_chip * 2 + core, c,
             )
-            move.start()
-            moves["chip", ch].append(move)
-
-    def sub_stage(ch):
-        for move in moves["chip", ch]:
-            move.wait_recv()
-        for m in range(2):
-            total = chip_acc[ch, chip, m]
+        factor_in[ch, pl.ds(chip, 1)] = factor_send[ch, pl.ds(chip, 1)]
+
+    def factor_sum(ch):
+        arrive(("factor", ch))
+        arrive(("known", ch))
+        total = dot(
+            factor_in[ch].reshape(chips * nodes, width // chips),
+            known[ch].reshape(chips * nodes, width), TN,
+        )
+        factor_part[ch] = total.reshape(2, block, width)
+        factor_out_s[ch] = factor_part[ch, 1 - core].astype(BF16)
+        start(
+            ("core", ch), factor_out_s.at[ch], factor_core.at[ch],
+            core_send.at[ch], core_recv.at[ch], other_core, c,
+        )
+
+    def core_stage(ch, grad):
+        m = ch - 2
+        part[m] = grad.reshape(2, half_rows, width)
+        core_out[m] = part[m, 1 - core].astype(BF16)
+        start(
+            ("core", ch), core_out.at[m], core_in.at[m],
+            core_send.at[ch], core_recv.at[ch], other_core, c,
+        )
+
+    def chip_stage(ch):
+        m = ch - 2
+        arrive(("core", ch))
+        for j in range(chips):
+            at = pl.ds(j * block, block)
+            total = part[m, core, at, :] + core_in[m, at, :].astype(F32)
+            chip_acc[m, j] = total
+            chip_out[m, j] = total.astype(BF16)
+        for j in range(1, chips):
+            to_chip = lax.rem(chip + j, chips)
+            start(
+                ("chip", ch), chip_out.at[m, to_chip], chip_in.at[m, j],
+                chip_send.at[m, j], chip_recv.at[m, j], to_chip * 2 + core, c,
+            )
+
+    def sub_step(ch, t):
+        keep = n_sub >> (t + 1)
+        low = 0
+        for earlier in range(t):
+            low = low + lax.rem(lax.div(c, 2**earlier), 2) * (n_sub >> (earlier + 1))
+        bit = lax.rem(lax.div(c, 2**t), 2)
+        for i in range(keep):
+            sub_out[ch, t, i] = sub_acc[ch, low + (1 - bit) * keep + i].astype(BF16)
+        start(
+            ("sub", ch, t), sub_out.at[ch, t, pl.ds(0, keep)], sub_in.at[ch, t, pl.ds(0, keep)],
+            sub_send.at[ch, t], sub_recv.at[ch, t], g, flip(c, 2**t),
+        )
+
+    def sub_sum(ch, t):
+        keep = n_sub >> (t + 1)
+        arrive(("sub", ch, t))
+        low = 0
+        for earlier in range(t + 1):
+            low = low + lax.rem(lax.div(c, 2**earlier), 2) * (n_sub >> (earlier + 1))
+        for i in range(keep):
+            sub_acc[ch, low + i] = sub_acc[ch, low + i] + sub_in[ch, t, i].astype(F32)
+
+    def sub_first(ch):
+        if ch < 2:
+            arrive(("core", ch))
+            total = factor_part[ch, core] + factor_core[ch].astype(F32)
+        else:
+            arrive(("chip", ch))
+            total = chip_acc[ch - 2, chip]
             for j in range(1, chips):
-                total = total + chip_in[ch, j, m].astype(F32)
-            for z in range(n_sub):
-                piece = total[:, z * (width // n_sub):(z + 1) * (width // n_sub)]
-                sub_acc[ch, z, m] = piece
-                sub_out[ch, z, m] = piece.astype(BF16)
-        moves["sub", ch] = []
-        for k in far_first[:-1]:
-            to_sub = lax.rem(c + k, n_sub)
-            move = remote(
-                sub_out.at[ch, to_sub], sub_in.at[ch, k],
-                sub_send.at[ch, k], sub_recv.at[ch, k], g, to_sub,
+                total = total + chip_in[ch - 2, j].astype(F32)
+        for z in range(n_sub):
+            sub_acc[ch, z] = total[:, z * lanes:(z + 1) * lanes]
+        sub_step(ch, 0)
+
+    def sub_next(ch):
+        for t in range(1, sub_bits):
+            sub_sum(ch, t - 1)
+            sub_step(ch, t)
+
+    def gather_step(ch, t):
+        held = n_sub >> (t + 1)
+        at_chip = chip_of[0] * (1 - part_of) + chip_of[1] * part_of
+        low = 0
+        for earlier in range(1, t + 1):
+            low = low + lax.rem(lax.div(c, 2**earlier), 2) * (n_sub >> (earlier + 1))
+        piece = whole.at[ch, part_of, at_chip, pl.ds(low, held)]
+        start(
+            ("subg", ch, t), piece, piece, subg_send.at[ch, t], subg_recv.at[ch, t],
+            g, flip(c, 2**t),
+        )
+
+    def sub_gather(ch):
+        t = sub_bits - 1
+        sub_sum(ch, t)
+        spot = reverse(c, sub_bits)
+        at_chip = chip_of[0] * (1 - part_of) + chip_of[1] * part_of
+        whole[ch, part_of, at_chip, pl.ds(lax.rem(spot, n_sub // 2), 1)] = (
+            sub_acc[ch, spot].astype(BF16)[None]
+        )
+        gather_step(ch, t)
+
+    def sub_gather_next(ch):
+        for t in range(sub_bits - 2, -1, -1):
+            arrive(("subg", ch, t + 1))
+            gather_step(ch, t)
+
+    def chip_step(ch, t):
+        for p in range(2):
+            bit = 2**t if p == 0 else 2 ** (chip_bits - 1 - t)
+            low = lax.div(chip_of[p], 2**t) * 2**t
+            piece = whole.at[ch, p, pl.ds(low, 2**t)]
+            start(
+                ("chipg", ch, t), piece, piece, chipg_send.at[ch, p, t], chipg_recv.at[ch, p, t],
+                flip(chip, bit) * 2 + core, c,
             )
-            move.start()
-            moves["sub", ch].append(move)
-
-    def sub_gather(ch):
-        for move in moves["sub", ch]:
-            move.wait_recv()
-        total = sub_acc[ch, c]
-        for k in range(1, n_sub):
-            total = total + sub_in[ch, k].astype(F32)
-        whole[ch, chip, pl.ds(c, 1)] = total.astype(BF16)[None]
-        moves["subg", ch] = []
-        for k in far_first[:-1]:
-            move = remote(
-                whole.at[ch, chip, c], whole.at[ch, chip, c],
-                subg_send.at[ch, k], subg_recv.at[ch, k], g, lax.rem(c + k, n_sub),
-            )
-            move.start()
-            moves["subg", ch].append(move)
 
     def chip_gather(ch):
-        for move in moves["subg", ch]:
-            move.wait_recv()
-        moves["chipg", ch] = []
-        for j in range(1, chips):
-            move = remote(
-                whole.at[ch, chip], whole.at[ch, chip],
-                chipg_send.at[ch, j], chipg_recv.at[ch, j],
-                lax.rem(chip + j, chips) * 2 + core, c,
-            )
-            move.start()
-            moves["chipg", ch].append(move)
+        arrive(("subg", ch, 0))
+        chip_step(ch, 0)
+
+    def chip_gather_next(ch):
+        for t in range(1, chip_bits):
+            arrive(("chipg", ch, t - 1))
+            chip_step(ch, t)
 
     def core_gather(ch):
-        for move in moves["chipg", ch]:
-            move.wait_recv()
-        move = remote(
-            whole.at[ch], gathered.at[ch, core], coreg_send.at[ch], coreg_recv.at[ch],
-            other_core, c,
-        )
-        move.start()
-        moves["coreg", ch] = [move]
+        arrive(("chipg", ch, chip_bits - 1))
+        start(
+            ("coreg", ch), whole.at[ch], gathered.at[ch, core],
+            coreg_send.at[ch], coreg_recv.at[ch], other_core, c,
+        )
         own = pltpu.make_async_copy(whole.at[ch], gathered.at[ch, core], store_sem.at[ch])
         own.start()
         stores.append(own)
 
-    stores = []
-    core_stage(0, dot(mn_s[...], qg_s[...], TN), dot(att_s[...], og_s[...], TN))
-    core_stage(1, dot(rows_in, back_k[...], TN), dot(rows_in, back_v[...], TN))
-    for ch in range(chunks):
-        chip_stage(ch)
-
+    moves.update(known_moves)
+    far, near = far_first[0], far_first[1:-1]
+    home = [(k, o) for k in (far, *near) for o in range(3)] + [(0, 0), (0, 2)]
+
+    def send_next():
+        if home:
+            send_home(*home.pop(0))
+
+    factor_out(0)
+    factor_out(1)
+    turn_back(far)
+    send_next()
+    core_stage(2, dot(rows_in, back_k[...], TN))
+    core_stage(3, dot(rows_in, back_v[...], TN))
+    factor_sum(0)
+    factor_sum(1)
+    chip_stage(2)
+    chip_stage(3)
+    sub_first(0)
+    sub_first(1)
+    send_next()
+    for k in (*near, 0):
+        turn_back(k)
+    returned[1, pl.ds(c, 1)] = slot_back[0, 1][None]
+    sub_next(0)
+    sub_next(1)
+    send_next()
     mo_s[...] = (mesh_wide + dot(att_s[...], wo_s[...])).astype(BF16)
     mesh_normed_grad = dot(qg_s[...], wq_s[...], NT)
     mg_s[...] = (
@@ -332,21 +448,30 @@
         own.start()
         stores.append(own)
 
-    for ch in range(chunks):
-        sub_stage(ch)
-    for ch in range(chunks):
-        sub_gather(ch)
-    for ch in range(chunks):
-        chip_gather(ch)
+    stages = (
+        (sub_first, 2), (sub_gather, 0), (sub_gather, 1), None,
+        (sub_first, 3), (sub_next, 2), (sub_gather_next, 0), (sub_gather_next, 1), None,
+        (sub_next, 3), (sub_gather, 2), (chip_gather, 0), (chip_gather, 1), None,
+        (sub_gather, 3), (sub_gather_next, 2), (chip_gather_next, 0), (chip_gather_next, 1), None,
+        (sub_gather_next, 3), (chip_gather, 2), None,
+        (chip_gather, 3), None, (chip_gather_next, 2), None,
+        (core_gather, 0), (core_gather, 1), None,
+        (chip_gather_next, 3), None, (core_gather, 2), (core_gather, 3),
+    )
+    for stage in stages:
+        if stage is None:
+            send_next()
+        else:
+            stage[0](stage[1])
+    while home:
+        send_next()
     for move in backward.values():
         move.wait_recv()
     own = pltpu.make_async_copy(returned, returned_out, store_sem.at[chunks + 2])
     own.start()
     stores.append(own)
     for ch in range(chunks):
-        core_gather(ch)
-    for ch in range(chunks):
-        moves["coreg", ch][0].wait_recv()
+        arrive(("coreg", ch))
     for own in stores:
         own.wait()
     for move in [*forward.values(), *backward.values()] + sum(moves.values(), []):
@@ -361,8 +486,8 @@
     points, width = x_s.shape
     n_sub, slots_per = rows_s.shape[2:]
     block = n_sub * slots_per
-    chunks, _, chips, _, mats, part_rows, part_lanes = gathered_s.shape
-    pieces = x_s.shape[0] // 4
+    chunks, _, _, chips, _, part_rows, part_lanes = gathered_s.shape
+    pieces = points // 4
     loads = {}
     pairs = [
         ("rows", rows, rows_s), ("gg", gain_g, gg_s), ("back", returned, returned_s),
@@ -406,17 +531,33 @@
     loads["mg"].wait()
     store(mg_s, mesh_grad)
     half_rows = width // 2
-    for ch, order in enumerate(((0, 3), (1, 2))):
+    chip_bits = chips.bit_length() - 1
+
+    def flipped(index, bits):
+        return sum((index >> t & 1) << (bits - 1 - t) for t in range(bits))
+
+    def piece_of(ch, core, j, z):
+        part, at = divmod(z, n_sub // 2)
+        return gathered_s[ch, core, part, flipped(j, chip_bits) if part else j, at].astype(F32)
+
+    for ch, matrix in enumerate((3, 0, 1, 2)):
         loads["w", ch].wait()
-        for m, matrix in enumerate(order):
-            for core in range(2):
-                for j in range(chips):
-                    at = core * half_rows + j * part_rows
-                    for z in range(n_sub):
-                        w_s[matrix, at:at + part_rows, z * part_lanes:(z + 1) * part_lanes] = (
-                            gathered_s[ch, core, j, z, m].astype(F32)
-                        )
-            store(w_s.at[matrix], weight_grads.at[matrix])
+        for j in range(chips):
+            for z in range(n_sub):
+                columns = slice(z * part_lanes, (z + 1) * part_lanes)
+                cores = [piece_of(ch, core, j, z) for core in range(2)]
+                if ch < 2:
+                    both = jnp.concatenate(cores, axis=0)
+                    span = slice(2 * j * part_rows, 2 * (j + 1) * part_rows)
+                    if ch == 0:
+                        w_s[matrix, span, columns] = both
+                    else:
+                        w_s[matrix, columns, span] = both.T
+                else:
+                    for core in range(2):
+                        at = core * half_rows + j * part_rows
+                        w_s[matrix, at:at + part_rows, columns] = cores[core]
+        store(w_s.at[matrix], weight_grads.at[matrix])
     for move in stores:
         move.wait()
 
@@ -432,7 +573,7 @@
     fanout = neighbours.shape[1]
     slots = 3 * n_sub * slots_per
     chips = n_grid // 2
-    chunks, mats = 2, 2
+    chunks = 4
     half_rows = width // 2
     block, lanes = half_rows // chips, width // n_sub
     anywhere = pl.BlockSpec(memory_space=pl.ANY)
@@ -446,14 +587,15 @@
     turns = (n_sub, 3, slots_per, width)
     node_rows = pltpu.VMEM((nodes, width), BF16)
     slot_rows = pltpu.VMEM((slots, width), BF16)
-    piece = (chunks, n_sub, mats, block, lanes)
+    chip_bits, sub_bits = chips.bit_length() - 1, n_sub.bit_length() - 1
+    pieces = (chunks, 2, 2, chips, n_sub // 2, block, lanes)
     returned, gathered, mesh_out, mesh_grad = pl.pallas_call(
         functools.partial(layer, n_grid, n_sub),
         in_specs=[anywhere] * len(operands),
         out_specs=[anywhere] * 4,
         out_shape=[
             jax.ShapeDtypeStruct(blocks, BF16),
-            jax.ShapeDtypeStruct((chunks, 2, chips, n_sub, mats, block, lanes), BF16),
+            jax.ShapeDtypeStruct(pieces, BF16),
             jax.ShapeDtypeStruct((nodes, width), BF16),
             jax.ShapeDtypeStruct((nodes, width), BF16),
         ],
@@ -463,23 +605,28 @@
             pltpu.VMEM((nodes * ROWS, LANES), F32),
             pltpu.VMEM((slots // LANES, nodes * 8, LANES), F32),
             pltpu.VMEM((nodes, fanout), jnp.int32),
-            node_rows, node_rows, node_rows, slot_rows, slot_rows, node_rows, node_rows,
+            node_rows, node_rows, slot_rows, slot_rows, node_rows, node_rows,
             slot_rows, slot_rows, node_rows, node_rows,
-            pltpu.VMEM((chunks, mats, 2, half_rows, width), F32),
-            pltpu.VMEM((chunks, mats, half_rows, width), BF16),
-            pltpu.VMEM((chunks, mats, half_rows, width), BF16),
-            pltpu.VMEM((chunks, chips, mats, block, width), F32),
-            pltpu.VMEM((chunks, chips, mats, block, width), BF16),
-            pltpu.VMEM((chunks, chips, mats, block, width), BF16),
-            pltpu.VMEM(piece, F32), pltpu.VMEM(piece, BF16), pltpu.VMEM(piece, BF16),
-            pltpu.VMEM((chunks, chips, n_sub, mats, block, lanes), BF16),
+            pltpu.VMEM((2, chips, nodes, width), BF16),
+            pltpu.VMEM((2, chips, nodes, width // chips), BF16),
+            pltpu.VMEM((2, chips, nodes, width // chips), BF16),
+            pltpu.VMEM((2, 2, block, width), F32),
+            pltpu.VMEM((2, block, width), BF16), pltpu.VMEM((2, block, width), BF16),
+            pltpu.VMEM((2, 2, half_rows, width), F32),
+            pltpu.VMEM((2, half_rows, width), BF16), pltpu.VMEM((2, half_rows, width), BF16),
+            pltpu.VMEM((2, chips, block, width), F32),
+            pltpu.VMEM((2, chips, block, width), BF16), pltpu.VMEM((2, chips, block, width), BF16),
+            pltpu.VMEM((chunks, n_sub, block, lanes), F32),
+            pltpu.VMEM((chunks, sub_bits, n_sub // 2, block, lanes), BF16),
+            pltpu.VMEM((chunks, sub_bits, n_sub // 2, block, lanes), BF16),
+            pltpu.VMEM(pieces[:1] + pieces[2:], BF16),
             dma((len(operands),)),
             dma((3 * n_sub,)), dma((3 * n_sub,)), dma((3 * n_sub,)), dma((3 * n_sub,)),
-            dma((chunks,)), dma((chunks,)),
-            dma((chunks, chips)), dma((chunks, chips)),
-            dma((chunks, n_sub)), dma((chunks, n_sub)),
-            dma((chunks, n_sub)), dma((chunks, n_sub)),
-            dma((chunks, chips)), dma((chunks, chips)),
+            dma((2, chips)), dma((2, chips)), dma((2, chips)), dma((2, chips)),
+            dma((chunks,)), dma((chunks,)), dma((2, chips)), dma((2, chips)),
+            dma((chunks, sub_bits)), dma((chunks, sub_bits)),
+            dma((chunks, sub_bits)), dma((chunks, sub_bits)),
+            dma((chunks, 2, chip_bits)), dma((chunks, 2, chip_bits)),
             dma((chunks,)), dma((chunks,)),
             dma((chunks + 3,)),
         ],
@@ -494,17 +641,17 @@
             jax.ShapeDtypeStruct((nodes, width), BF16),
             jax.ShapeDtypeStruct((nodes, width), BF16),
             jax.ShapeDtypeStruct((points, width), BF16),
-            jax.ShapeDtypeStruct((chunks * mats, width, width), F32),
+            jax.ShapeDtypeStruct((chunks, width, width), F32),
         ],
         scratch_shapes=[
             pltpu.VMEM(blocks, BF16),
-            pltpu.VMEM((chunks, 2, chips, n_sub, mats, block, lanes), BF16),
+            pltpu.VMEM(pieces, BF16),
             node_rows, node_rows,
             pltpu.VMEM((points, width), BF16), pltpu.VMEM((1, width), F32),
             pltpu.VMEM(send_rows.shape, jnp.int32), pltpu.VMEM((1, slots), jnp.int32),
             pltpu.VMEM((points, width), BF16),
-            pltpu.VMEM((chunks * mats, width, width), F32),
-            dma((9 + chunks,)), dma((6 + chunks * mats,)),
+            pltpu.VMEM((chunks, width, width), F32),
+            dma((9 + chunks,)), dma((6 + chunks,)),
         ],
         name="finish",
     )(returned, gathered, mesh_out, mesh_grad, grid_x, gain_grid, send_rows)

time: 81.7 us -> 74.6 us (0.913)
  Pallas kernels: 80.8 us -> 73.7 us
    pallas_call x1, Pallas kernels: 74.6 us -> 67.6 us  [shards(): pl.pallas_call(functools.partial(layer, n_grid, n_sub), in_specs=[anywher...]
where the time goes in v2:
time: 74.6 us; the launch traced here: 74.4 us
  Pallas kernels  73.7 us (99%)
    pallas_call x1, Pallas kernels, shards(): pl.pallas_call(functools.partial(layer, n_grid, n_sub), in_specs=[anywher...  67.6 us
    pallas_call x1, Pallas kernels, shards(): pl.pallas_call(finish, in_specs=[anywhere] * 7, out_specs=[anywhere] * 4,...  6.16 us

profile of v2, /device:TPU:0, one launch (start us, length us, event | category | flops | bytes accessed | tf_op | source)
XLA Modules:
  0.0 74.4 jit_solution(14528097023639373842)
XLA Ops:
  0.6 67.6 %layer.1 = (bf16[3,4,64,512]{3,2,1,0:T(8,128)(2,1)}, bf16[4,2,2,4,2,64,128]{6,5,4,3,2,1,0:T(8,128)(2,1)}, bf16[64,512]{1,0:T(8,128)(2,1)}, bf16[64,512]{1,0:T(8,128)(2,1)}) custom-call(bf16[2048,512]{1,0:T(8,128)(2,1)} %grid_x.3, bf16[64,512]{1,0:T(8,128)(2,1)} %mesh_h.1, f32[1,512]{1,0:T(1,128)} %bitcast.2, f32[1,512]{1,0:T(1,128)} %bitcast.4, ...), custom_call_target="tpu_custom_call" | custom-call | tf_op jit(solution)/shard_map/layer/pallas_call | solution.py:592
  68.2 6.2 %finish.1 = (bf16[64,512]{1,0:T(8,128)(2,1)}, bf16[64,512]{1,0:T(8,128)(2,1)}, bf16[2048,512]{1,0:T(8,128)(2,1)}, f32[4,512,512]{2,1,0:T(8,128)}) custom-call(bf16[3,4,64,512]{3,2,1,0:T(8,128)(2,1)} %get-tuple-element.8.returned, bf16[4,2,2,4,2,64,128]{6,5,4,3,2,1,0:T(8,128)(2,1)} %get-tuple-element.9.gathered, ...), custom_call_target="tpu_custom_call" | custom-call | tf_op jit(solution)/shard_map/finish/pallas_call | solution.py:636

commit v3 on v2

v3 whole, which is shorter than its diff:
```python
import functools

import jax
import jax.numpy as jnp
from jax import lax
from jax.experimental import pallas as pl
from jax.experimental.pallas import tpu as pltpu
from jax.sharding import PartitionSpec as P

EPSILON = 1e-06
NEG_FILL = -1e30
F32 = jnp.float32
BF16 = jnp.bfloat16
NN = (((1,), (0,)), ((), ()))
NT = (((1,), (1,)), ((), ()))
TN = (((0,), (0,)), ((), ()))
LANES = 128
LIMIT = 32 * 2**20
VMEM_BYTES = 67043328
ROWS = 24


def dot(a, b, dims=NN):
    return lax.dot_general(a, b, dims, preferred_element_type=F32)


def normalize(values_in, gain_row):
    widened = values_in.astype(F32)
    factor = lax.rsqrt(jnp.mean(widened * widened, axis=-1, keepdims=True) + EPSILON)
    return (widened, factor, (widened * factor * gain_row).astype(BF16))


def normalize_back(widened, factor, gain_row, upstream):
    scaled = gain_row * upstream
    inner_mean = jnp.mean(widened * scaled, axis=-1, keepdims=True)
    return factor * scaled - widened * factor**3 * inner_mean


def layer(
    n_grid,
    n_sub,
    grid_x, mesh_h, gain_g, gain_m, w_q, w_k, w_v, w_o, bias, nbr, valid, rows, out_grad,
    grid_grad, gathered, mgathered, mo_s, mg_s,
    x_s, mesh_s, gg_s, gm_s, wq_s, wk_s, wv_s, wo_s, bias_s, nbr_s, valid_s, rows_s, og_s,
    packet, arrived, rows_t, slot_back, returned, flat, onehot_t, factor_s,
    edge_rows, dense, slot_of, q_s, ag_s, k_s, v_s, att_s, qg_s, back_k, back_v,
    known, factor_send, factor_in, factor_part, factor_out_s, factor_core,
    part, core_out, core_in, chip_acc, chip_out, chip_in,
    msub_acc, msub_out, msub_in, mwhole, sub_acc, sub_out, sub_in, whole,
    load_sem, fwd_send, fwd_recv, back_send, back_recv,
    known_send, known_recv, factor_ssem, factor_rsem, core_send, core_recv,
    mcore_send, mcore_recv, chip_send, chip_recv, msub_send, msub_recv,
    msubg_send, msubg_recv, mchipg_send, mchipg_recv, mcoreg_send, mcoreg_recv,
    sub_send, sub_recv,
    subg_send, subg_recv, chipg_send, chipg_recv, coreg_send, coreg_recv,
):
    g = lax.axis_index("grid")
    c = lax.axis_index("sub")
    core = lax.rem(g, 2)
    chip = lax.div(g, 2)
    chips = n_grid // 2
    other_core = g + 1 - 2 * core
    points, width = x_s.shape
    nodes = mesh_s.shape[0]
    slots_per = rows_s.shape[3]
    fanout = nbr_s.shape[1]
    heads = bias_s.shape[1] // fanout
    head = width // heads
    slots = 3 * n_sub * slots_per
    scale = head ** (-0.5)
    half = points // 2

    loads = {}
    pairs = (
        ("rows", rows, rows_s), ("x", grid_x, x_s), ("gg", gain_g, gg_s), ("nbr", nbr, nbr_s),
        ("bias", bias, bias_s), ("valid", valid, valid_s), ("mesh", mesh_h, mesh_s),
        ("gm", gain_m, gm_s), ("wq", w_q, wq_s), ("og", out_grad, og_s), ("wo", w_o, wo_s),
        ("wk", w_k, wk_s), ("wv", w_v, wv_s),
    )
    for at, (name, source, target) in enumerate(pairs):
        loads[name] = pltpu.make_async_copy(source, target, load_sem.at[at])
        loads[name].start()

    def wrap(value, size):
        return lax.rem(value + size, size)

    def remote(source, target, send, recv, to_grid, to_sub):
        return pltpu.make_async_remote_copy(
            src_ref=source, dst_ref=target, send_sem=send, recv_sem=recv,
            device_id={"grid": to_grid, "sub": to_sub}, device_id_type=pl.DeviceIdType.MESH,
        )

    barrier = pltpu.get_barrier_semaphore()
    peers = [
        (wrap(g + o, n_grid), wrap(c + k, n_sub))
        for k in range(n_sub) for o in (-1, 0, 1) if (o, k) != (0, 0)
    ] + [(lax.rem(chip + j, chips) * 2 + core, c) for j in range(1, chips)]
    for to_grid, to_sub in peers:
        pl.semaphore_signal(
            barrier, inc=1, device_id={"grid": to_grid, "sub": to_sub},
            device_id_type=pl.DeviceIdType.MESH,
        )

    far_first = sorted(range(n_sub), key=lambda k: -min(k, n_sub - k))

    loads["rows"].wait()
    eye = (
        lax.broadcasted_iota(jnp.int32, (slots_per, slots_per), 0)
        == lax.broadcasted_iota(jnp.int32, (slots_per, slots_per), 1)
    )
    forward = {}
    for o in (0, 2, 1):
        low, span = (0, half) if o == 0 else (half, points - half) if o == 2 else (0, points)
        lane = lax.broadcasted_iota(jnp.int32, (slots_per, span), 1) + low
        picks = []
        for s in range(n_sub):
            row = rows_s[0, o, pl.ds(s, 1), :].astype(F32)
            column = jnp.sum(jnp.where(eye, row, 0.0), axis=1, keepdims=True).astype(jnp.int32)
            picks.append(jnp.where(lane == column, 1.0, 0.0).astype(BF16))
        onehot = jnp.concatenate(picks, axis=0)
        if o == 0:
            loads["x"].wait()
            loads["gg"].wait()
        chosen = dot(onehot, x_s[pl.ds(low, span), :])
        factor = lax.rsqrt(jnp.mean(chosen * chosen, axis=-1, keepdims=True) + EPSILON)
        packet[o] = (chosen * factor * gg_s[...]).astype(BF16).reshape(n_sub, slots_per, width)
        if o == 0:
            pl.semaphore_wait(barrier, len(peers))
        for k in far_first:
            if (o, k) == (1, 0):
                continue
            to_sub = lax.rem(c + k, n_sub)
            forward[o, k] = remote(
                packet.at[o, to_sub], arrived.at[o, k],
                fwd_send.at[o * n_sub + k], fwd_recv.at[o * n_sub + k],
                wrap(g + o - 1, n_grid), to_sub,
            )
            forward[o, k].start()
    arrived[1, 0] = packet[1, c]

    for name in ("mesh", "gm", "og"):
        loads[name].wait()
    mesh_wide, mesh_factor, mesh_normed = normalize(mesh_s[...], gm_s[...])
    known[0, pl.ds(chip, 1)] = og_s[...][None]
    known[1, pl.ds(chip, 1)] = mesh_normed[None]
    known_moves = {}
    for ch in range(2):
        known_moves["known", ch] = []
        for j in range(1, chips):
            to_chip = lax.rem(chip + j, chips)
            move = remote(
                known.at[ch, chip], known.at[ch, chip], known_send.at[ch, j], known_recv.at[ch, j],
                to_chip * 2 + core, c,
            )
            move.start()
            known_moves["known", ch].append(move)

    for name in ("nbr", "bias", "valid"):
        loads[name].wait()
    named = nbr_s[...]
    offset_of = lax.div(named, n_sub * slots_per)
    sub_of = lax.rem(lax.div(named, slots_per), n_sub)
    turn = lax.rem(c - sub_of + n_sub, n_sub)
    slot_of[...] = (offset_of * n_sub + turn) * slots_per + lax.rem(named, slots_per)
    edge_rows[...] = jnp.zeros(edge_rows.shape, F32)
    for h in range(heads):
        values = bias_s[:, h * fanout:(h + 1) * fanout]
        high = values.astype(BF16).astype(F32)
        middle = (values - high).astype(BF16).astype(F32)
        edge_rows[pl.ds(h, nodes, stride=ROWS), :fanout] = high
        edge_rows[pl.ds(8 + h, nodes, stride=ROWS), :fanout] = middle
        edge_rows[pl.ds(16 + h, nodes, stride=ROWS), :fanout] = values - high - middle
    edge_rows[pl.ds(heads, nodes, stride=ROWS), :fanout] = jnp.where(valid_s[...] == 1, 1.0, 0.0)

    slot_ids = lax.broadcasted_iota(jnp.int32, (slots, fanout), 0)
    group = 8

    def spread(step, carry):
        for inner in range(group):
            node = step * group + inner
            names = slot_ids == slot_of[pl.ds(node, 1), :]
            onehot = jnp.where(names, 1.0, 0.0).astype(BF16)
            at = pl.multiple_of(node * ROWS, 8)
            spread_rows = dot(edge_rows[pl.ds(at, ROWS), :fanout].astype(BF16), onehot, NT)
            total = (spread_rows[16:24] + spread_rows[8:16]) + spread_rows[:8]
            for tile in range(slots // LANES):
                dense[tile, pl.ds(pl.multiple_of(node * 8, 8), 8), :] = (
                    total[:, tile * LANES:(tile + 1) * LANES]
                )
        return carry

    lax.fori_loop(0, nodes // group, spread, 0)

    for o in range(3):
        for s in range(n_sub):
            at = (o * n_sub + s) * slots_per
            flat[:, at:at + slots_per] = rows_s[0, o, pl.ds(s, 1), :]
    block_rows = n_sub * slots_per
    for h in range(2):
        point = lax.broadcasted_iota(jnp.int32, (half, 2 * block_rows), 0) + h * half
        names = point == flat[:, h * block_rows:(h + 2) * block_rows]
        onehot_t[h] = jnp.where(names, 1.0, 0.0).astype(BF16)
    tile = half // 2
    for b in range(4):
        wide = x_s[b * tile:(b + 1) * tile, :].astype(F32)
        factor_s[b * tile:(b + 1) * tile, :] = lax.rsqrt(
            jnp.mean(wide * wide, axis=-1, keepdims=True) + EPSILON
        )

    for name in ("wq", "wo", "wk", "wv"):
        loads[name].wait()
    q_s[...] = (dot(mesh_normed, wq_s[...]) * scale).astype(BF16)
    ag_s[...] = dot(og_s[...], wo_s[...], NT).astype(BF16)

    for o in (0, 2, 1):
        for k in range(n_sub):
            if (o, k) != (1, 0):
                forward[o, k].wait_recv()
        here = slice(o * n_sub * slots_per, (o + 1) * n_sub * slots_per)
        rows_in = arrived[o].reshape(n_sub * slots_per, width)
        rows_t[:, here] = rows_in.T
        k_s[here, :] = dot(rows_in, wk_s[...]).astype(BF16)
        v_s[here, :] = dot(rows_in, wv_s[...]).astype(BF16)

    def spread_of(row):
        return jnp.concatenate(
            [dense[tile, pl.ds(row, nodes, stride=8), :] for tile in range(slots // LANES)], axis=1
        )

    live = spread_of(heads) > 0.5
    for h in range(heads):
        mine = slice(h * head, (h + 1) * head)
        queries, keys, values, att_grad = q_s[:, mine], k_s[:, mine], v_s[:, mine], ag_s[:, mine]
        scores = dot(queries, keys, NT) + spread_of(h)
        peak = jnp.max(jnp.where(live, scores, NEG_FILL), axis=1, keepdims=True)
        terms = jnp.exp(jnp.where(live, scores - peak, NEG_FILL))
        probs = terms / jnp.sum(terms, axis=1, keepdims=True)
        probs_b = probs.astype(BF16)
        att_s[:, mine] = dot(probs_b, values).astype(BF16)
        prob_grads = dot(att_grad, values, NT)
        score_grads = (
            probs * (prob_grads - jnp.sum(probs * prob_grads, axis=1, keepdims=True))
        ).astype(BF16)
        qg_s[:, mine] = (dot(score_grads, keys) * scale).astype(BF16)
        back_k[:, mine] = dot(score_grads, queries, TN).astype(BF16)
        back_v[:, mine] = dot(probs_b, att_grad, TN).astype(BF16)

    backward = {}

    def turn_back(o):
        here = slice(o * n_sub * slots_per, (o + 1) * n_sub * slots_per)
        total = dot(back_k[here, :], wk_s[...], NT) + dot(back_v[here, :], wv_s[...], NT)
        slot_back[o] = total.astype(BF16).reshape(n_sub, slots_per, width)

    def send_home(o, k):
        backward[o, k] = remote(
            slot_back.at[o, k], returned.at[o, c],
            back_send.at[o * n_sub + k], back_recv.at[o * n_sub + k],
            wrap(g + 1 - o, n_grid), wrap(c - k, n_sub),
        )
        backward[o, k].start()

    half_rows = width // 2
    chunks = whole.shape[0]
    block = half_rows // chips
    lanes = width // n_sub
    chip_bits = chips.bit_length() - 1
    moves = {}

    def flip(index, bit):
        return index + bit - 2 * bit * lax.rem(lax.div(index, bit), 2)

    def reverse(index, bits):
        total = 0
        for t in range(bits):
            total = total + lax.rem(lax.div(index, 2**t), 2) * 2 ** (bits - 1 - t)
        return total

    chip_of = (chip, reverse(chip, chip_bits))

    def start(key, *move):
        moves.setdefault(key, []).append(remote(*move))
        moves[key][-1].start()

    def arrive(key):
        for move in moves[key]:
            move.wait_recv()

    def factor_out(ch):
        source = (att_s, qg_s)[ch]
        piece = width // chips
        for j in range(chips):
            factor_send[ch, j] = source[:, j * piece:(j + 1) * piece]
        for j in range(1, chips):
            to_chip = lax.rem(chip + j, chips)
            start(
                ("factor", ch), factor_send.at[ch, to_chip], factor_in.at[ch, chip],
                factor_ssem.at[ch, j], factor_rsem.at[ch, j], to_chip * 2 + core, c,
            )
        factor_in[ch, pl.ds(chip, 1)] = factor_send[ch, pl.ds(chip, 1)]

    def factor_sum(ch):
        arrive(("factor", ch))
        arrive(("known", ch))
        total = dot(
            factor_in[ch].reshape(chips * nodes, width // chips),
            known[ch].reshape(chips * nodes, width), TN,
        )
        factor_part[ch] = total.reshape(2, block, width)
        factor_out_s[ch] = factor_part[ch, 1 - core].astype(BF16)
        start(
            ("core", ch), factor_out_s.at[ch], factor_core.at[ch],
            core_send.at[ch], core_recv.at[ch], other_core, c,
        )

    quarter_rows = half_rows // 2
    part_rows = quarter_rows // chips
    thirds = [k for k in far_first if k]

    def core_stage(m, grad):
        part[m] = grad.reshape(2, quarter_rows, width)
        core_out[m] = part[m, 1 - core].astype(BF16)
        start(
            ("mcore", m), core_out.at[m], core_in.at[m],
            mcore_send.at[m], mcore_recv.at[m], other_core, c,
        )

    def chip_stage(m):
        arrive(("mcore", m))
        for j in range(chips):
            at = pl.ds(j * part_rows, part_rows)
            total = part[m, core, at, :] + core_in[m, at, :].astype(F32)
            chip_acc[m, j] = total
            chip_out[m, j] = total.astype(BF16)
        for j in range(1, chips):
            to_chip = lax.rem(chip + j, chips)
            start(
                ("mchip", m), chip_out.at[m, to_chip], chip_in.at[m, j],
                chip_send.at[m, j], chip_recv.at[m, j], to_chip * 2 + core, c,
            )

    def sub_stage(m):
        arrive(("mchip", m))
        total = chip_acc[m, chip]
        for j in range(1, chips):
            total = total + chip_in[m, j].astype(F32)
        for z in range(n_sub):
            piece = total[:, z * lanes:(z + 1) * lanes]
            msub_acc[m, z] = piece
            msub_out[m, z] = piece.astype(BF16)
        for k in thirds:
            to_sub = lax.rem(c + k, n_sub)
            start(
                ("msub", m), msub_out.at[m, to_sub], msub_in.at[m, k],
                msub_send.at[m, k], msub_recv.at[m, k], g, to_sub,
            )

    def sub_spread(m):
        arrive(("msub", m))
        total = msub_acc[m, c]
        for k in range(1, n_sub):
            total = total + msub_in[m, k].astype(F32)
        mwhole[m, chip, pl.ds(c, 1)] = total.astype(BF16)[None]
        piece = mwhole.at[m, chip, c]
        for k in thirds:
            start(
                ("msubg", m), piece, piece, msubg_send.at[m, k], msubg_recv.at[m, k],
                g, lax.rem(c + k, n_sub),
            )

    def chip_spread(m):
        arrive(("msubg", m))
        piece = mwhole.at[m, chip]
        for j in range(1, chips):
            start(
                ("mchipg", m), piece, piece, mchipg_send.at[m, j], mchipg_recv.at[m, j],
                lax.rem(chip + j, chips) * 2 + core, c,
            )

    def core_spread(m):
        arrive(("mchipg", m))
        start(
            ("mcoreg", m), mwhole.at[m], mgathered.at[m, core],
            mcoreg_send.at[m], mcoreg_recv.at[m], other_core, c,
        )
        mgathered[m, pl.ds(core, 1)] = mwhole[m][None]

    def sub_first(ch):
        arrive(("core", ch))
        total = factor_part[ch, core] + factor_core[ch].astype(F32)
        for z in range(n_sub):
            piece = total[:, z * lanes:(z + 1) * lanes]
            sub_acc[ch, z] = piece
            sub_out[ch, z] = piece.astype(BF16)
        for k in thirds:
            to_sub = lax.rem(c + k, n_sub)
            start(
                ("sub", ch), sub_out.at[ch, to_sub], sub_in.at[ch, k],
                sub_send.at[ch, k], sub_recv.at[ch, k], g, to_sub,
            )

    def sub_gather(ch):
        arrive(("sub", ch))
        total = sub_acc[ch, c]
        for k in range(1, n_sub):
            total = total + sub_in[ch, k].astype(F32)
        p = lax.div(c, n_sub // 2)
        at_chip = chip_of[0] * (1 - p) + chip_of[1] * p
        spot = lax.rem(c, n_sub // 2)
        whole[ch, p, at_chip, pl.ds(spot, 1)] = total.astype(BF16)[None]
        piece = whole.at[ch, p, at_chip, spot]
        for k in thirds:
            start(
                ("subg", ch), piece, piece, subg_send.at[ch, k], subg_recv.at[ch, k],
                g, lax.rem(c + k, n_sub),
            )

    def chip_step(ch, t):
        for p in range(2):
            bit = 2**t if p == 0 else 2 ** (chip_bits - 1 - t)
            low = lax.div(chip_of[p], 2**t) * 2**t
            piece = whole.at[ch, p, pl.ds(low, 2**t)]
            start(
                ("chipg", ch, t), piece, piece, chipg_send.at[ch, p, t], chipg_recv.at[ch, p, t],
                flip(chip, bit) * 2 + core, c,
            )

    def chip_gather(ch):
        arrive(("subg", ch))
        chip_step(ch, 0)

    def chip_gather_next(ch):
        for t in range(1, chip_bits):
            arrive(("chipg", ch, t - 1))
            chip_step(ch, t)

    def core_gather(ch):
        arrive(("chipg", ch, chip_bits - 1))
        start(
            ("coreg", ch), whole.at[ch], gathered.at[ch, core],
            coreg_send.at[ch], coreg_recv.at[ch], other_core, c,
        )
        gathered[ch, pl.ds(core, 1)] = whole[ch][None]

    moves.update(known_moves)
    home = [(o, k) for o in (0, 2, 1) for k in far_first if (o, k) != (1, 0)]

    def send_next(count=1):
        for _ in range(min(count, len(home))):
            send_home(*home.pop(0))

    def nodes_out():
        mo_s[...] = (mesh_wide + dot(att_s[...], wo_s[...])).astype(BF16)
        mesh_normed_grad = dot(qg_s[...], wq_s[...], NT)
        mg_s[...] = (
            og_s[...].astype(F32)
            + normalize_back(mesh_wide, mesh_factor, gm_s[...], mesh_normed_grad)
        ).astype(BF16)

    def stage_of_matrix(m):
        span = slice(m % 2 * half_rows, (m % 2 + 1) * half_rows)
        core_stage(m, dot(rows_t[span, :], (back_k, back_v)[m // 2][...]))

    for stage, *of in (
        (factor_out, 0), (factor_out, 1), (turn_back, 0), (send_next, 3),
        (stage_of_matrix, 0), (stage_of_matrix, 1), (stage_of_matrix, 2), (stage_of_matrix, 3),
        (factor_sum, 0), (factor_sum, 1),
        (chip_stage, 0), (chip_stage, 1), (chip_stage, 2), (chip_stage, 3),
        (sub_first, 0), (sub_first, 1), (turn_back, 2), (send_next, 3), (turn_back, 1), (nodes_out,),
        (sub_gather, 0), (sub_gather, 1),
        (sub_stage, 0), (sub_stage, 1), (sub_stage, 2), (sub_spread, 0),
        (chip_gather, 0), (chip_gather, 1),
        (sub_stage, 3), (sub_spread, 1), (sub_spread, 2), (sub_spread, 3), (send_next, 1),
        (chip_gather_next, 0), (chip_gather_next, 1), (send_next, 1),
        (chip_spread, 0), (chip_spread, 1), (send_next, 1),
        (chip_spread, 2), (chip_spread, 3), (send_next, 2),
        (core_gather, 0), (core_gather, 1),
        (core_spread, 0), (core_spread, 1), (core_spread, 2), (core_spread, 3),
    ):
        stage(*of)
    returned[1, pl.ds(c, 1)] = slot_back[1, 0][None]
    send_next(len(home))
    for move in backward.values():
        move.wait_recv()
    for b in range(4):
        h, at = b // 2, slice(b * tile, (b + 1) * tile)
        home_rows = returned[h:h + 2].reshape(2 * block_rows, width)
        normed_grad = dot(onehot_t[h, b % 2 * tile:(b % 2 + 1) * tile, :], home_rows)
        wide = x_s[at, :].astype(F32)
        grid_grad[at, :] = normalize_back(
            wide, factor_s[at, :], gg_s[...], normed_grad
        ).astype(BF16)
    for ch in range(chunks):
        arrive(("coreg", ch))
    for m in range(4):
        arrive(("mcoreg", m))
    for move in [*forward.values(), *backward.values()] + sum(moves.values(), []):
        move.wait_send()


def finish(
    gathered_s, mgathered_s, mo_s, mg_s, gx_s, mesh_out, mesh_grad, grid_grad, weight_grads,
    w_s, store_sem,
):
    width = gx_s.shape[1]
    half_rows = width // 2
    chunks, _, _, chips, halves, part_rows, part_lanes = gathered_s.shape
    n_sub = 2 * halves
    stores = []

    def store(source, target):
        move = pltpu.make_async_copy(source, target, store_sem.at[len(stores)])
        move.start()
        stores.append(move)

    store(gx_s, grid_grad)
    store(mo_s, mesh_out)
    store(mg_s, mesh_grad)
    chip_bits = chips.bit_length() - 1

    def flipped(index, bits):
        return sum((index >> t & 1) << (bits - 1 - t) for t in range(bits))

    def piece_of(ch, core, j, z):
        part, at = divmod(z, n_sub // 2)
        return gathered_s[ch, core, part, flipped(j, chip_bits) if part else j, at].astype(F32)

    for ch, matrix in enumerate((3, 0)):
        for j in range(chips):
            for z in range(n_sub):
                columns = slice(z * part_lanes, (z + 1) * part_lanes)
                span = slice(2 * j * part_rows, 2 * (j + 1) * part_rows)
                both = jnp.concatenate([piece_of(ch, core, j, z) for core in range(2)], axis=0)
                if ch == 0:
                    w_s[matrix, span, columns] = both
                else:
                    w_s[matrix, columns, span] = both.T
        store(w_s.at[matrix], weight_grads.at[matrix])
    for m in range(4):
        rows_of = part_rows // 2
        for core in range(2):
            for j in range(chips):
                at = m % 2 * half_rows + core * half_rows // 2 + j * rows_of
                for z in range(n_sub):
                    columns = slice(z * part_lanes, (z + 1) * part_lanes)
                    w_s[1 + m // 2, at:at + rows_of, columns] = mgathered_s[m, core, j, z].astype(F32)
        at = pl.ds(m % 2 * half_rows, half_rows)
        store(w_s.at[1 + m // 2, at], weight_grads.at[1 + m // 2, at])
    for move in stores:
        move.wait()


def shards(
    n_grid, n_sub,
    grid_x, mesh_h, gain_grid, gain_mesh, w_query, w_key, w_value, w_out,
    edge_bias, neighbours, valid, send_rows, out_grad,
):
    points, width = grid_x.shape
    nodes = mesh_h.shape[0]
    slots_per = send_rows.shape[3]
    fanout = neighbours.shape[1]
    slots = 3 * n_sub * slots_per
    chips = n_grid // 2
    chunks = 2
    half_rows = width // 2
    block, lanes = half_rows // chips, width // n_sub
    anywhere = pl.BlockSpec(memory_space=pl.ANY)
    inside = pl.BlockSpec(memory_space=pltpu.VMEM)
    dma = pltpu.SemaphoreType.DMA
    gain_grid, gain_mesh = gain_grid.reshape(1, width), gain_mesh.reshape(1, width)
    operands = (
        grid_x, mesh_h, gain_grid, gain_mesh, w_query, w_key, w_value, w_out,
        edge_bias, neighbours, valid, send_rows, out_grad,
    )
    blocks = (3, n_sub, slots_per, width)
    node_rows = pltpu.VMEM((nodes, width), BF16)
    slot_rows = pltpu.VMEM((slots, width), BF16)
    chip_bits = chips.bit_length() - 1
    pieces = (chunks, 2, 2, chips, n_sub // 2, block, lanes)
    mpieces = (4, 2, chips, n_sub, block // 2, lanes)
    kept = 2 * (points * width + 2 * nodes * width + 4 * width * width) + 2**16
    found = pl.pallas_call(
        functools.partial(layer, n_grid, n_sub),
        in_specs=[anywhere] * len(operands),
        out_specs=[inside] * 5,
        out_shape=[
            pltpu.VMEM((points, width), BF16),
            pltpu.VMEM(pieces, BF16),
            pltpu.VMEM(mpieces, BF16),
            node_rows, node_rows,
        ],
        scratch_shapes=[pltpu.VMEM(a.shape, a.dtype) for a in operands] + [
            pltpu.VMEM(blocks, BF16), pltpu.VMEM(blocks, BF16), pltpu.VMEM((width, slots), BF16),
            pltpu.VMEM(blocks, BF16), pltpu.VMEM(blocks, BF16), pltpu.VMEM((1, slots), jnp.int32),
            pltpu.VMEM((2, points // 2, 2 * n_sub * slots_per), BF16), pltpu.VMEM((points, 1), F32),
            pltpu.VMEM((nodes * ROWS, LANES), F32),
            pltpu.VMEM((slots // LANES, nodes * 8, LANES), F32),
            pltpu.VMEM((nodes, fanout), jnp.int32),
            node_rows, node_rows, slot_rows, slot_rows, node_rows, node_rows,
            slot_rows, slot_rows,
            pltpu.VMEM((2, chips, nodes, width), BF16),
            pltpu.VMEM((2, chips, nodes, width // chips), BF16),
            pltpu.VMEM((2, chips, nodes, width // chips), BF16),
            pltpu.VMEM((2, 2, block, width), F32),
            pltpu.VMEM((2, block, width), BF16), pltpu.VMEM((2, block, width), BF16),
            pltpu.VMEM((4, 2, half_rows // 2, width), F32),
            pltpu.VMEM((4, half_rows // 2, width), BF16), pltpu.VMEM((4, half_rows // 2, width), BF16),
            pltpu.VMEM((4, chips, block // 2, width), F32),
            pltpu.VMEM((4, chips, block // 2, width), BF16),
            pltpu.VMEM((4, chips, block // 2, width), BF16),
            pltpu.VMEM((4, n_sub, block // 2, lanes), F32),
            pltpu.VMEM((4, n_sub, block // 2, lanes), BF16),
            pltpu.VMEM((4, n_sub, block // 2, lanes), BF16),
            pltpu.VMEM(mpieces[:1] + mpieces[2:], BF16),
            pltpu.VMEM((chunks, n_sub, block, lanes), F32),
            pltpu.VMEM((chunks, n_sub, block, lanes), BF16),
            pltpu.VMEM((chunks, n_sub, block, lanes), BF16),
            pltpu.VMEM(pieces[:1] + pieces[2:], BF16),
            dma((len(operands),)),
            dma((3 * n_sub,)), dma((3 * n_sub,)), dma((3 * n_sub,)), dma((3 * n_sub,)),
            dma((2, chips)), dma((2, chips)), dma((2, chips)), dma((2, chips)),
            dma((chunks,)), dma((chunks,)),
            dma((4,)), dma((4,)), dma((4, chips)), dma((4, chips)), dma((4, n_sub)), dma((4, n_sub)),
            dma((4, n_sub)), dma((4, n_sub)), dma((4, chips)), dma((4, chips)), dma((4,)), dma((4,)),
            dma((chunks, n_sub)), dma((chunks, n_sub)),
            dma((chunks, n_sub)), dma((chunks, n_sub)),
            dma((chunks, 2, chip_bits)), dma((chunks, 2, chip_bits)),
            dma((chunks,)), dma((chunks,)),
        ],
        compiler_params=pltpu.CompilerParams(
            collective_id=0, has_side_effects=True, vmem_limit_bytes=VMEM_BYTES - kept
        ),
        name="layer",
    )(*operands)
    gx, gathered, mgathered, mo, mg = found
    return pl.pallas_call(
        finish,
        in_specs=[inside] * 5,
        out_specs=[anywhere] * 4,
        out_shape=[
            jax.ShapeDtypeStruct((nodes, width), BF16),
            jax.ShapeDtypeStruct((nodes, width), BF16),
            jax.ShapeDtypeStruct((points, width), BF16),
            jax.ShapeDtypeStruct((4, width, width), F32),
        ],
        scratch_shapes=[pltpu.VMEM((4, width, width), F32), dma((9,))],
        compiler_params=pltpu.CompilerParams(vmem_limit_bytes=LIMIT),
        name="finish",
    )(gathered, mgathered, mo, mg, gx)


def solution(mesh):
    by_device = P(("grid", "sub"), None)
    in_specs = (
        by_device, by_device, P(), P(), P(), P(), P(), P(), by_device, by_device, by_device,
        P(("grid", "sub"), None, None, None), by_device,
    )
    out_specs = (by_device, by_device, by_device, P())
    body = functools.partial(shards, mesh.shape["grid"], mesh.shape["sub"])
    return jax.shard_map(body, mesh=mesh, in_specs=in_specs, out_specs=out_specs, check_vma=False)
```

time: 74.6 us -> 71.6 us (0.960)
  Pallas kernels: 73.7 us -> 70.7 us
    pallas_call x1, Pallas kernels: 6.16 us -> 2.77 us  [shards(): pl.pallas_call(finish, in_specs=[inside] * 5, out_specs=[anywhere] * 4, o...]
where the time goes in v3:
time: 71.6 us; the launch traced here: 71.4 us
  Pallas kernels  70.7 us (99%)
    pallas_call x1, Pallas kernels, shards(): pl.pallas_call(functools.partial(layer, n_grid, n_sub), in_specs=[anywher...  67.9 us
    pallas_call x1, Pallas kernels, shards(): pl.pallas_call(finish, in_specs=[inside] * 5, out_specs=[anywhere] * 4, o...  2.77 us

profile of v3, /device:TPU:0, one launch (start us, length us, event | category | flops | bytes accessed | tf_op | source)
XLA Modules:
  0.0 71.4 jit_solution(7431440256531441968)
XLA Ops:
  0.6 67.9 %layer.1 = (bf16[2048,512]{1,0:T(8,128)(2,1)S(1)}, bf16[2,2,2,4,2,64,128]{6,5,4,3,2,1,0:T(8,128)(2,1)S(1)}, bf16[4,2,4,4,32,128]{5,4,3,2,1,0:T(8,128)(2,1)S(1)},...) custom-call(bf16[2048,512]{1,0:T(8,128)(2,1)} %grid_x.1, bf16[64,512]{1,0:T(8,128)(2,1)} %mesh_h.1, f32[1,512]{1,0:T(1,128)} %bitcast.2, ...), custom_call_target="tpu_custom_call" | custom-call | tf_op jit(solution)/shard_map/layer/pallas_call | solution.py:582
  68.6 2.8 %finish.1 = (bf16[64,512]{1,0:T(8,128)(2,1)}, bf16[64,512]{1,0:T(8,128)(2,1)}, bf16[2048,512]{1,0:T(8,128)(2,1)}, f32[4,512,512]{2,1,0:T(8,128)}) custom-call(bf16[2,2,2,4,2,64,128]{6,5,4,3,2,1,0:T(8,128)(2,1)S(1)} %get-tuple-element.9.gathered_s, bf16[4,2,4,4,32,128]{5,4,3,2,1,0:T(8,128)(2,1)S(1)} %get-tuple-element.10.mgathered_s, ...), custom_call_target="tpu_custom_call" | custom-call | tf_op jit(solution)/shard_map/finish/pallas_call | solution.py:636

commit v4 on v3

--- a/solution.py
+++ b/solution.py
@@ -70,6 +70,26 @@
     scale = head ** (-0.5)
     half = points // 2
 
+    def wrap(value, size):
+        return lax.rem(value + size, size)
+
+    def remote(source, target, send, recv, to_grid, to_sub):
+        return pltpu.make_async_remote_copy(
+            src_ref=source, dst_ref=target, send_sem=send, recv_sem=recv,
+            device_id={"grid": to_grid, "sub": to_sub}, device_id_type=pl.DeviceIdType.MESH,
+        )
+
+    barrier = pltpu.get_barrier_semaphore()
+    peers = [
+        (wrap(g + o, n_grid), wrap(c + k, n_sub))
+        for k in range(n_sub) for o in (-1, 0, 1) if (o, k) != (0, 0)
+    ] + [(lax.rem(chip + j, chips) * 2 + core, c) for j in range(1, chips)]
+    for to_grid, to_sub in peers:
+        pl.semaphore_signal(
+            barrier, inc=1, device_id={"grid": to_grid, "sub": to_sub},
+            device_id_type=pl.DeviceIdType.MESH,
+        )
+
     loads = {}
     pairs = (
         ("rows", rows, rows_s), ("x", grid_x, x_s), ("gg", gain_g, gg_s), ("nbr", nbr, nbr_s),
@@ -80,26 +100,6 @@
     for at, (name, source, target) in enumerate(pairs):
         loads[name] = pltpu.make_async_copy(source, target, load_sem.at[at])
         loads[name].start()
-
-    def wrap(value, size):
-        return lax.rem(value + size, size)
-
-    def remote(source, target, send, recv, to_grid, to_sub):
-        return pltpu.make_async_remote_copy(
-            src_ref=source, dst_ref=target, send_sem=send, recv_sem=recv,
-            device_id={"grid": to_grid, "sub": to_sub}, device_id_type=pl.DeviceIdType.MESH,
-        )
-
-    barrier = pltpu.get_barrier_semaphore()
-    peers = [
-        (wrap(g + o, n_grid), wrap(c + k, n_sub))
-        for k in range(n_sub) for o in (-1, 0, 1) if (o, k) != (0, 0)
-    ] + [(lax.rem(chip + j, chips) * 2 + core, c) for j in range(1, chips)]
-    for to_grid, to_sub in peers:
-        pl.semaphore_signal(
-            barrier, inc=1, device_id={"grid": to_grid, "sub": to_sub},
-            device_id_type=pl.DeviceIdType.MESH,
-        )
 
     far_first = sorted(range(n_sub), key=lambda k: -min(k, n_sub - k))
 
@@ -251,6 +251,8 @@
         here = slice(o * n_sub * slots_per, (o + 1) * n_sub * slots_per)
         total = dot(back_k[here, :], wk_s[...], NT) + dot(back_v[here, :], wv_s[...], NT)
         slot_back[o] = total.astype(BF16).reshape(n_sub, slots_per, width)
+        if o == 1:
+            returned[1, pl.ds(c, 1)] = slot_back[1, 0][None]
 
     def send_home(o, k):
         backward[o, k] = remote(
@@ -266,9 +268,6 @@
     lanes = width // n_sub
     chip_bits = chips.bit_length() - 1
     moves = {}
-
-    def flip(index, bit):
-        return index + bit - 2 * bit * lax.rem(lax.div(index, bit), 2)
 
     def reverse(index, bits):
         total = 0
@@ -415,27 +414,18 @@
                 g, lax.rem(c + k, n_sub),
             )
 
-    def chip_step(ch, t):
-        for p in range(2):
-            bit = 2**t if p == 0 else 2 ** (chip_bits - 1 - t)
-            low = lax.div(chip_of[p], 2**t) * 2**t
-            piece = whole.at[ch, p, pl.ds(low, 2**t)]
-            start(
-                ("chipg", ch, t), piece, piece, chipg_send.at[ch, p, t], chipg_recv.at[ch, p, t],
-                flip(chip, bit) * 2 + core, c,
-            )
-
     def chip_gather(ch):
         arrive(("subg", ch))
-        chip_step(ch, 0)
-
-    def chip_gather_next(ch):
-        for t in range(1, chip_bits):
-            arrive(("chipg", ch, t - 1))
-            chip_step(ch, t)
+        for p in range(2):
+            piece = whole.at[ch, p, chip_of[p]]
+            for j in range(1, chips):
+                start(
+                    ("chipg", ch), piece, piece, chipg_send.at[ch, p, j], chipg_recv.at[ch, p, j],
+                    lax.rem(chip + j, chips) * 2 + core, c,
+                )
 
     def core_gather(ch):
-        arrive(("chipg", ch, chip_bits - 1))
+        arrive(("chipg", ch))
         start(
             ("coreg", ch), whole.at[ch], gathered.at[ch, core],
             coreg_send.at[ch], coreg_recv.at[ch], other_core, c,
@@ -457,32 +447,10 @@
             + normalize_back(mesh_wide, mesh_factor, gm_s[...], mesh_normed_grad)
         ).astype(BF16)
 
-    def stage_of_matrix(m):
-        span = slice(m % 2 * half_rows, (m % 2 + 1) * half_rows)
-        core_stage(m, dot(rows_t[span, :], (back_k, back_v)[m // 2][...]))
-
-    for stage, *of in (
-        (factor_out, 0), (factor_out, 1), (turn_back, 0), (send_next, 3),
-        (stage_of_matrix, 0), (stage_of_matrix, 1), (stage_of_matrix, 2), (stage_of_matrix, 3),
-        (factor_sum, 0), (factor_sum, 1),
-        (chip_stage, 0), (chip_stage, 1), (chip_stage, 2), (chip_stage, 3),
-        (sub_first, 0), (sub_first, 1), (turn_back, 2), (send_next, 3), (turn_back, 1), (nodes_out,),
-        (sub_gather, 0), (sub_gather, 1),
-        (sub_stage, 0), (sub_stage, 1), (sub_stage, 2), (sub_spread, 0),
-        (chip_gather, 0), (chip_gather, 1),
-        (sub_stage, 3), (sub_spread, 1), (sub_spread, 2), (sub_spread, 3), (send_next, 1),
-        (chip_gather_next, 0), (chip_gather_next, 1), (send_next, 1),
-        (chip_spread, 0), (chip_spread, 1), (send_next, 1),
-        (chip_spread, 2), (chip_spread, 3), (send_next, 2),
-        (core_gather, 0), (core_gather, 1),
-        (core_spread, 0), (core_spread, 1), (core_spread, 2), (core_spread, 3),
-    ):
-        stage(*of)
-    returned[1, pl.ds(c, 1)] = slot_back[1, 0][None]
-    send_next(len(home))
-    for move in backward.values():
-        move.wait_recv()
-    for b in range(4):
+    def grid_rows(b):
+        if b == 0:
+            for move in backward.values():
+                move.wait_recv()
         h, at = b // 2, slice(b * tile, (b + 1) * tile)
         home_rows = returned[h:h + 2].reshape(2 * block_rows, width)
         normed_grad = dot(onehot_t[h, b % 2 * tile:(b % 2 + 1) * tile, :], home_rows)
@@ -490,6 +458,25 @@
         grid_grad[at, :] = normalize_back(
             wide, factor_s[at, :], gg_s[...], normed_grad
         ).astype(BF16)
+
+    def stage_of_matrix(m):
+        span = slice(m % 2 * half_rows, (m % 2 + 1) * half_rows)
+        core_stage(m, dot(rows_t[span, :], (back_k, back_v)[m // 2][...]))
+
+    for stage, *of in (
+        (factor_out, 0), (factor_out, 1), (turn_back, 0), (send_next, 3), (stage_of_matrix, 0),
+        (stage_of_matrix, 1), (stage_of_matrix, 2), (stage_of_matrix, 3), (factor_sum, 0),
+        (factor_sum, 1), (chip_stage, 0), (chip_stage, 1), (chip_stage, 2), (chip_stage, 3),
+        (sub_first, 0), (sub_first, 1), (turn_back, 2), (send_next, 1), (turn_back, 1),
+        (nodes_out,), (sub_gather, 0), (sub_gather, 1), (sub_stage, 0), (sub_stage, 1),
+        (sub_stage, 2), (sub_stage, 3), (send_next, 1), (chip_gather, 0), (chip_gather, 1),
+        (sub_spread, 0), (send_next, 1), (sub_spread, 1), (send_next, 1), (sub_spread, 2),
+        (send_next, 1), (sub_spread, 3), (send_next, 3), (chip_spread, 0), (chip_spread, 1),
+        (chip_spread, 2), (chip_spread, 3), (core_gather, 0), (core_gather, 1), (grid_rows, 0),
+        (grid_rows, 1), (grid_rows, 2), (grid_rows, 3), (core_spread, 0), (core_spread, 1),
+        (core_spread, 2), (core_spread, 3),
+    ):
+        stage(*of)
     for ch in range(chunks):
         arrive(("coreg", ch))
     for m in range(4):
@@ -624,7 +611,7 @@
             dma((4, n_sub)), dma((4, n_sub)), dma((4, chips)), dma((4, chips)), dma((4,)), dma((4,)),
             dma((chunks, n_sub)), dma((chunks, n_sub)),
             dma((chunks, n_sub)), dma((chunks, n_sub)),
-            dma((chunks, 2, chip_bits)), dma((chunks, 2, chip_bits)),
+            dma((chunks, 2, chips)), dma((chunks, 2, chips)),
             dma((chunks,)), dma((chunks,)),
         ],
         compiler_params=pltpu.CompilerParams(

time: 71.6 us -> 69.5 us (0.971)
  Pallas kernels: 70.7 us -> 68.6 us
    pallas_call x1, Pallas kernels: 67.9 us -> 65.9 us  [shards(): pl.pallas_call(functools.partial(layer, n_grid, n_sub), in_specs=[anywher...]
where the time goes in v4:
time: 69.5 us; the launch traced here: 69.3 us
  Pallas kernels  68.6 us (99%)
    pallas_call x1, Pallas kernels, shards(): pl.pallas_call(functools.partial(layer, n_grid, n_sub), in_specs=[anywher...  65.9 us
    pallas_call x1, Pallas kernels, shards(): pl.pallas_call(finish, in_specs=[inside] * 5, out_specs=[anywhere] * 4, o...  2.77 us

profile of v4, /device:TPU:0, one launch (start us, length us, event | category | flops | bytes accessed | tf_op | source)
XLA Modules:
  0.0 69.3 jit_solution(13724412332780281370)
XLA Ops:
  0.6 65.9 %layer.1 = (bf16[2048,512]{1,0:T(8,128)(2,1)S(1)}, bf16[2,2,2,4,2,64,128]{6,5,4,3,2,1,0:T(8,128)(2,1)S(1)}, bf16[4,2,4,4,32,128]{5,4,3,2,1,0:T(8,128)(2,1)S(1)},...) custom-call(bf16[2048,512]{1,0:T(8,128)(2,1)} %grid_x.1, bf16[64,512]{1,0:T(8,128)(2,1)} %mesh_h.1, f32[1,512]{1,0:T(1,128)} %bitcast.2, ...), custom_call_target="tpu_custom_call" | custom-call | tf_op jit(solution)/shard_map/layer/pallas_call | solution.py:569
  66.5 2.8 %finish.1 = (bf16[64,512]{1,0:T(8,128)(2,1)}, bf16[64,512]{1,0:T(8,128)(2,1)}, bf16[2048,512]{1,0:T(8,128)(2,1)}, f32[4,512,512]{2,1,0:T(8,128)}) custom-call(bf16[2,2,2,4,2,64,128]{6,5,4,3,2,1,0:T(8,128)(2,1)S(1)} %get-tuple-element.9.gathered_s, bf16[4,2,4,4,32,128]{5,4,3,2,1,0:T(8,128)(2,1)S(1)} %get-tuple-element.10.mgathered_s, ...), custom_call_target="tpu_custom_call" | custom-call | tf_op jit(solution)/shard_map/finish/pallas_call | solution.py:623
